TPU v7x, 32 devices: a whole 2x2x4 slice. The times are simulated.
32 devices in a mesh: gx: 2 (over core), gy: 4 (over y, x), gz: 4 (over z).
Axes of the slice: x: 2, y: 2, z: 4, core: 2. Of those that a mesh axis runs over, the one named last changes fastest.
Arguments:
- raw_weight: float32 [128, 27, 128], P(('gx', 'gy')), may hold values from -6 to 6
- inputs: bfloat16 [16, 64, 64, 128], P('gx', 'gy', 'gz'), may hold values from -6 to 6
- cotangent: bfloat16 [16, 64, 64, 128], P('gx', 'gy', 'gz'), may hold values from -0.099609375 to 0.099609375
Outputs:
- input_grad: bfloat16 [16, 64, 64, 128], P('gx', 'gy', 'gz')
- weight_grad: float32 [128, 27, 128], P(('gx', 'gy'))
All inputs are finite; a program needn't handle non-finite values.
Results may differ from a plain program's by a relative error of at most 0.0049.
Values may be sent and summed in bfloat16 or wider, within the bound.
A program may use at most 64 MiB of HBM per device.

v0:
```python
import functools

import jax
import jax.numpy as jnp
from jax import lax
from jax.experimental import pallas as pl
from jax.experimental.pallas import tpu as pltpu
from jax.sharding import PartitionSpec as P

var_eps = 1e-05
norm_eps = 1e-06
clip_norm = 600.0
F32 = jnp.float32
BF16 = jnp.bfloat16
MESH = pl.DeviceIdType.MESH
AXES = ("gx", "gy", "gz")


def z_groups(taps, nz):
    chunk = taps // 3
    sizes = [-(-2 * chunk // nz), -(-chunk // nz)]
    return [(0, 0, 2 * chunk, sizes[0]), (sizes[0] * nz, 2 * chunk, chunk, sizes[1])]


def kernel(dims, raw_hbm, in_hbm, cot_hbm, dx_ref, wg_ref, *scratch):
    (raw_ref, in_ref, shifted, face_out, face_in, in_t, part, recv_x, send_y, recv_y, send_z, recv_z, full, std,
     std_all, w_cat, stats, stats_in, total_in, load_sem, halo_send, halo_recv, x_send, x_recv, y_send, y_recv,
     z_send, z_recv, g_send, g_recv, ay_send, ay_recv, ax_send, ax_recv, st_send, st_recv, t_send, t_recv) = scratch
    count = dict(zip(AXES, dims))
    nx, ny, nz = dims
    plane_peers = nx * ny - 1
    me = {axis: lax.axis_index(axis) for axis in AXES}
    taps, rows, chan = raw_ref.shape
    ex, ey, ez = in_ref.shape[:3]
    chunk = taps // 3
    groups = z_groups(taps, nz)
    fan_count = float(rows * nx * ny * taps)

    def peer(axis, k):
        return lax.rem(me[axis] + k, count[axis])

    def plane_peer(k):
        flat = lax.rem(me["gx"] * ny + me["gy"] + k, nx * ny)
        return {"gx": lax.div(flat, ny), "gy": lax.rem(flat, ny)}

    def remote(src, dst, send_sem, recv_sem, where):
        return pltpu.make_async_remote_copy(
            src_ref=src, dst_ref=dst, send_sem=send_sem, recv_sem=recv_sem,
            device_id=where, device_id_type=MESH,
        )

    def wait_all(copies):
        for copy in copies:
            copy.wait()

    body = pl.ds(1, ey)
    load_raw = pltpu.make_async_copy(raw_hbm, raw_ref, load_sem.at[0])
    load_cot = pltpu.make_async_copy(cot_hbm, shifted.at[1, pl.ds(1, ex), body], load_sem.at[1])
    load_in = pltpu.make_async_copy(in_hbm, in_ref, load_sem.at[2])
    load_raw.start()
    load_cot.start()
    load_in.start()

    barrier = pltpu.get_barrier_semaphore()
    for k in range(1, nx * ny):
        pl.semaphore_signal(barrier, inc=1, device_id=plane_peer(k), device_id_type=MESH)
    for k in range(1, nz):
        pl.semaphore_signal(barrier, inc=1, device_id={"gz": peer("gz", k)}, device_id_type=MESH)

    def exchange_start(slot, base, peers):
        copies = []
        for k, where in enumerate(peers):
            copy = remote(stats.at[slot], stats_in.at[base + k], st_send.at[base + k], st_recv.at[base + k], where)
            copy.start()
            copies.append(copy)
        return copies

    def exchange_sum(slot, base, copies):
        wait_all(copies)
        total = stats[slot]
        for k in range(len(copies)):
            total = total + stats_in[base + k]
        return total

    zero_plane = jnp.zeros((ey + 2, ez, chan), BF16)
    zero_col = jnp.zeros((ex + 2, ez, chan), BF16)
    zero_face = jnp.zeros((ex + 2, ey + 2, chan), BF16)

    @pl.when(me["gx"] == 0)
    def _():
        shifted[1, 0] = zero_plane

    @pl.when(me["gx"] == nx - 1)
    def _():
        shifted[1, ex + 1] = zero_plane

    @pl.when(me["gy"] == 0)
    def _():
        shifted[1, :, 0] = zero_col

    @pl.when(me["gy"] == ny - 1)
    def _():
        shifted[1, :, ey + 1] = zero_col

    @pl.when(me["gz"] == 0)
    def _():
        face_in[0] = zero_face

    @pl.when(me["gz"] == nz - 1)
    def _():
        face_in[1] = zero_face

    for t in [b + v for b, first, many, size in groups for v in range(many, size * nz)]:
        send_z[t] = jnp.zeros((rows, chan), BF16)
        std[t] = jnp.zeros((rows, chan), F32)

    load_raw.wait()

    def per_output(value):
        return jnp.sum(jnp.sum(value, axis=0), axis=0, keepdims=True)

    raw = raw_ref[...]
    stats[0] = jnp.concatenate([per_output(raw), per_output(raw * raw), jnp.zeros((6, chan), F32)], axis=0)
    pl.semaphore_wait(barrier, plane_peers + nz - 1)
    weight_sums = exchange_start(0, 0, [plane_peer(k) for k in range(1, nx * ny)])
    load_cot.wait()

    def halo(axis, number, low_src, high_dst, high_src, low_dst):
        lower, upper = lax.max(me[axis] - 1, 0), lax.min(me[axis] + 1, count[axis] - 1)
        down = remote(low_src, high_dst, halo_send.at[2 * number], halo_recv.at[2 * number], {axis: lower})
        up = remote(high_src, low_dst, halo_send.at[2 * number + 1], halo_recv.at[2 * number + 1], {axis: upper})

        @pl.when(me[axis] > 0)
        def _():
            down.start()

        @pl.when(me[axis] < count[axis] - 1)
        def _():
            up.start()

        def finish():
            @pl.when(me[axis] > 0)
            def _():
                down.wait_send()
                up.wait_recv()

            @pl.when(me[axis] < count[axis] - 1)
            def _():
                up.wait_send()
                down.wait_recv()

        return finish

    def inside(dx, dy):
        gx, gy = me["gx"] + dx, me["gy"] + dy
        within = jnp.logical_and(gx >= 0, gx < nx)
        return jnp.logical_and(within, jnp.logical_and(gy >= 0, gy < ny))

    plane_halo = []
    for dx, dy in [(0, -1), (0, 1), (-1, 0), (1, 0), (-1, -1), (-1, 1), (1, -1), (1, 1)]:
        src_x = {-1: 1, 0: pl.ds(1, ex), 1: ex}[dx]
        dst_x = {-1: ex + 1, 0: pl.ds(1, ex), 1: 0}[dx]
        src_y = {-1: 1, 0: body, 1: ey}[dy]
        dst_y = {-1: ey + 1, 0: body, 1: 0}[dy]
        where = {
            "gx": lax.min(lax.max(me["gx"] + dx, 0), nx - 1),
            "gy": lax.min(lax.max(me["gy"] + dy, 0), ny - 1),
        }
        number = 2 + len(plane_halo)
        copy = remote(shifted.at[1, src_x, src_y], shifted.at[1, dst_x, dst_y],
                      halo_send.at[number], halo_recv.at[number], where)
        pl.when(inside(dx, dy))(copy.start)
        plane_halo.append((dx, dy, copy))
    load_in.wait()
    for x in range(ex):
        in_t[:, x * ey * ez:(x + 1) * ey * ez] = in_ref[x].reshape(ey * ez, chan).T
    for dx, dy, copy in plane_halo:
        pl.when(inside(dx, dy))(copy.wait_send)
        pl.when(inside(-dx, -dy))(copy.wait_recv)
    for x in range(ex + 2):
        plane = shifted[1, x].astype(F32)
        face_out[0, x] = plane[:, 0, :].astype(BF16)
        face_out[1, x] = plane[:, ez - 1, :].astype(BF16)
    halo_z = halo("gz", 0, face_out.at[0], face_in.at[1], face_out.at[1], face_in.at[0])

    sums = exchange_sum(0, 0, weight_sums)
    mean_out = sums[0:1] / fan_count
    var_out = sums[1:2] / fan_count - mean_out * mean_out
    inv_std = lax.rsqrt(var_out + var_eps)
    order = [t for c in (1, 0, 2) for t in range(c, taps, 3)]
    slots = [b + v for b, first, many, size in groups for v in range(many)]
    own = std_all.at[me["gx"], me["gy"]]
    for u, t in enumerate(order):
        value = (raw_ref[t] - mean_out) * inv_std
        std[slots[u]] = value
        own[u] = value.astype(BF16)
    gather_y = []
    for k in range(1, ny):
        copy = remote(own, own, ay_send.at[k - 1], ay_recv.at[k - 1], {"gy": peer("gy", k)})
        copy.start()
        gather_y.append(copy)

    def view(t, start, planes):
        a, b, c = t // 9, (t // 3) % 3, t % 3
        block = shifted[2 - c, pl.ds(start + 2 - a, planes), 2 - b:2 - b + ey]
        return block.reshape(planes * ey * ez, chan)

    def filter_chunk(n):
        for u in range(n * chunk, (n + 1) * chunk, 2):
            group = list(range(u, min(u + 2, (n + 1) * chunk)))
            views = [view(order[v], 0, ex) for v in group]
            right = jnp.concatenate(views, axis=1) if len(views) > 1 else views[0]
            product = jnp.dot(in_t[...], right, preferred_element_type=F32)
            for j, v in enumerate(group):
                for gx in range(nx):
                    for gy in range(ny):
                        low = (gx * ny + gy) * rows
                        part[gx, gy, v] = product[low:low + rows, j * chan:(j + 1) * chan]
        copies = []
        span = pl.ds(n * chunk, chunk)
        for k in range(1, nx):
            index = n * (nx - 1) + k - 1
            copy = remote(part.at[peer("gx", k), :, span], recv_x.at[k - 1, :, span],
                          x_send.at[index], x_recv.at[index], {"gx": peer("gx", k)})
            copy.start()
            copies.append(copy)
        return copies

    def rows_chunk(n, copies):
        wait_all(copies)
        span = pl.ds(n * chunk, chunk)
        for gy in range(ny):
            total = part[me["gx"], gy, span]
            for k in range(1, nx):
                total = total + recv_x[k - 1, gy, span]
            send_y[gy, span] = total.astype(BF16)
        sent = []
        for k in range(1, ny):
            index = n * (ny - 1) + k - 1
            copy = remote(send_y.at[peer("gy", k), span], recv_y.at[k - 1, span],
                          y_send.at[index], y_recv.at[index], {"gy": peer("gy", k)})
            copy.start()
            sent.append(copy)
        return sent

    depth_index = lax.broadcasted_iota(jnp.int32, (ey + 2, ez, chan), 1)

    def shift(slot, side, amount, edge):
        for x in range(ex + 2):
            plane = shifted[1, x].astype(F32)
            outer = face_in[side, x].astype(F32)[:, None, :]
            shifted[slot, x] = jnp.where(depth_index == edge, outer, pltpu.roll(plane, amount, 1)).astype(BF16)

    copies_0 = filter_chunk(0)
    halo_z()
    shift(2, 1, ez - 1, ez - 1)
    copies_1 = filter_chunk(1)
    reduce_y = [rows_chunk(0, copies_0)]
    shift(0, 0, 1, 0)
    copies_2 = filter_chunk(2)
    reduce_y.append(rows_chunk(1, copies_1))
    reduce_y.append(rows_chunk(2, copies_2))
    wait_all(gather_y)
    gather_x = []
    for k in range(1, nx):
        copy = remote(std_all.at[me["gx"]], std_all.at[me["gx"]], ax_send.at[k - 1], ax_recv.at[k - 1],
                      {"gx": peer("gx", k)})
        copy.start()
        gather_x.append(copy)

    step = 2 if ex % 2 == 0 else 1

    def dx_step(n, carry):
        start = n * step
        left = jnp.concatenate([view(t, start, step) for t in order], axis=1)
        product = lax.dot_general(left, w_cat[...], (((1,), (1,)), ((), ())), preferred_element_type=F32)
        dx_ref[pl.ds(start, step)] = product.astype(BF16).reshape(step, ey, ez, chan)
        return carry

    steps = ex // step
    half = steps // 2

    def depth_start(g):
        base, first, many, size = groups[g]
        span = pl.ds(first, many)
        total = send_y[me["gy"], span].astype(F32)
        for k in range(1, ny):
            total = total + recv_y[k - 1, span].astype(F32)
        send_z[base:base + many] = total.astype(BF16)
        copies = []
        for k in range(1, nz):
            index = g * (nz - 1) + k - 1
            copy = remote(send_z.at[pl.ds(base + peer("gz", k) * size, size)],
                          recv_z.at[k - 1, pl.ds(base // nz, size)],
                          z_send.at[index], z_recv.at[index], {"gz": peer("gz", k)})
            copy.start()
            copies.append(copy)
        return copies

    def depth_sum(g, copies):
        wait_all(copies)
        base, first, many, size = groups[g]
        mine = pl.ds(base + me["gz"] * size, size)
        grad = send_z[mine].astype(F32)
        for k in range(1, nz):
            grad = grad + recv_z[k - 1, pl.ds(base // nz, size)].astype(F32)
        full[mine] = grad.astype(BF16)
        sums = [per_output(grad), per_output(grad * std[mine]), per_output(grad * grad)]
        return jnp.concatenate(sums + [jnp.zeros((5, chan), F32)], axis=0)

    def gather_start(g):
        base, first, many, size = groups[g]
        mine = pl.ds(base + me["gz"] * size, size)
        copies = []
        for k in range(1, nz):
            index = g * (nz - 1) + k - 1
            copy = remote(full.at[mine], full.at[mine], g_send.at[index], g_recv.at[index], {"gz": peer("gz", k)})
            copy.start()
            copies.append(copy)
        return copies

    wait_all(reduce_y[0] + reduce_y[1])
    reduce_0 = depth_start(0)
    wait_all(gather_x)
    for u in range(taps):
        w_cat[:, u * chan:(u + 1) * chan] = std_all[:, :, u].reshape(nx * ny * rows, chan)
    lax.fori_loop(0, half, dx_step, 0)
    wait_all(reduce_y[2])
    reduce_1 = depth_start(1)
    lax.fori_loop(half, steps, dx_step, 0)
    first_sums = depth_sum(0, reduce_0)
    gather_z = gather_start(0)
    stats[1] = first_sums + depth_sum(1, reduce_1)
    flat = (me["gx"] * ny + me["gy"]) * nz + me["gz"]
    total_in[flat] = stats[1]
    final_sums = []
    for k in range(1, nx * ny * nz):
        other = lax.rem(flat + k, nx * ny * nz)
        where = {
            "gx": lax.div(other, ny * nz),
            "gy": lax.rem(lax.div(other, nz), ny),
            "gz": lax.rem(other, nz),
        }
        copy = remote(stats.at[1], total_in.at[flat], t_send.at[k - 1], t_recv.at[k - 1], where)
        copy.start()
        final_sums.append(copy)
    gather_z += gather_start(1)
    wait_all(final_sums)
    sums = total_in[0]
    for k in range(1, nx * ny * nz):
        sums = sums + total_in[k]
    wait_all(gather_z)
    sum_grad, sum_cross, sum_square = sums[0:1], sums[1:2], sums[2:3]
    mean_grad = sum_grad / fan_count
    mean_cross = sum_cross / fan_count
    spread = sum_square - 2.0 * mean_grad * sum_grad - 2.0 * mean_cross * sum_cross
    spread = (
        spread
        + fan_count * mean_grad * mean_grad
        + fan_count * mean_cross * mean_cross * var_out / (var_out + var_eps)
    )
    square_sum = jnp.sum(inv_std * inv_std * spread, axis=1, keepdims=True)
    scale = jnp.minimum(1.0, clip_norm * lax.rsqrt(square_sum + norm_eps))
    factor = inv_std * scale
    for u, t in enumerate(order):
        value = full[slots[u]].astype(F32)
        wg_ref[t] = factor * (value - mean_grad - std[slots[u]] * mean_cross)


def on_device(dims, raw_weight, inputs, cotangent):
    nx, ny, nz = dims
    rows, taps, chan = raw_weight.shape
    ex, ey, ez = inputs.shape[:3]
    groups = z_groups(taps, nz)
    piece = sum(size for base, first, many, size in groups)
    padded_taps = piece * nz
    stat_slots = nx * ny - 1
    dma = pltpu.SemaphoreType.DMA

    def pair(n):
        return [dma((max(n, 1),)), dma((max(n, 1),))]

    scratch = [
        pltpu.VMEM((taps, rows, chan), F32),
        pltpu.VMEM(inputs.shape, BF16),
        pltpu.VMEM((3, ex + 2, ey + 2, ez, chan), BF16),
        pltpu.VMEM((2, ex + 2, ey + 2, chan), BF16),
        pltpu.VMEM((2, ex + 2, ey + 2, chan), BF16),
        pltpu.VMEM((chan, ex * ey * ez), BF16),
        pltpu.VMEM((nx, ny, taps, rows, chan), F32),
        pltpu.VMEM((nx - 1, ny, taps, rows, chan), F32),
        pltpu.VMEM((ny, taps, rows, chan), BF16),
        pltpu.VMEM((ny - 1, taps, rows, chan), BF16),
        pltpu.VMEM((padded_taps, rows, chan), BF16),
        pltpu.VMEM((nz - 1, piece, rows, chan), BF16),
        pltpu.VMEM((padded_taps, rows, chan), BF16),
        pltpu.VMEM((padded_taps, rows, chan), F32),
        pltpu.VMEM((nx, ny, taps, rows, chan), BF16),
        pltpu.VMEM((chan, taps * chan), BF16),
        pltpu.VMEM((2, 8, chan), F32),
        pltpu.VMEM((stat_slots, 8, chan), F32),
        pltpu.VMEM((nx * ny * nz, 8, chan), F32),
        dma((3,)), *pair(10), *pair(3 * (nx - 1)), *pair(3 * (ny - 1)), *pair(2 * (nz - 1)), *pair(2 * (nz - 1)),
        *pair(ny - 1), *pair(nx - 1), *pair(stat_slots), *pair(nx * ny * nz - 1),
    ]
    vmem = pl.BlockSpec(memory_space=pltpu.VMEM)
    anywhere = pl.BlockSpec(memory_space=pl.ANY)
    input_grad, weight_grad = pl.pallas_call(
        functools.partial(kernel, dims),
        out_shape=(
            jax.ShapeDtypeStruct(cotangent.shape, BF16),
            jax.ShapeDtypeStruct((taps, rows, chan), F32),
        ),
        in_specs=[anywhere] * 3,
        out_specs=(vmem, vmem),
        scratch_shapes=scratch,
        compiler_params=pltpu.CompilerParams(
            collective_id=0, has_side_effects=True, vmem_limit_bytes=60 * 1024 * 1024
        ),
    )(jnp.transpose(raw_weight, (1, 0, 2)), inputs, cotangent)
    return input_grad, jnp.transpose(weight_grad, (1, 0, 2))


def solution(mesh):
    dims = tuple(mesh.shape[axis] for axis in AXES)
    in_specs = (P(("gx", "gy"), None, None), P("gx", "gy", "gz", None), P("gx", "gy", "gz", None))
    out_specs = (P("gx", "gy", "gz", None), P(("gx", "gy"), None, None))
    return jax.shard_map(
        functools.partial(on_device, dims), mesh=mesh, in_specs=in_specs, out_specs=out_specs, check_vma=False
    )
```

profile of v0, /device:TPU:0, one launch (start us, length us, event | category | flops | bytes accessed | tf_op | source)
XLA Modules:
  0.0 37.5 jit_solution(5211112686576529303)
XLA Ops:
  0.6 34.2 %shard_map.50 = (bf16[8,16,16,128]{3,2,1,0:T(8,128)(2,1)}, f32[27,16,128]{2,1,0:T(8,128)}) custom-call(f32[27,16,128]{2,1,0:T(8,128)} %bitcast.2, bf16[8,16,16,128]{3,2,1,0:T(8,128)(2,1)} %in_hbm.1, bf16[8,16,16,128]{3,2,1,0:T(8,128)(2,1)} %cot_hbm.1), custom_call_target="tpu_custom_call" | custom-call | tf_op jit(solution)/shard_map/pallas_call | solution.py:408
  34.9 0.0 copy-start
  34.9 1.9 %copy.7 = bf16[8,16,16,128]{3,2,1,0:T(8,128)(2,1)} copy(bf16[8,16,16,128]{3,2,1,0:T(8,128)(2,1)} %get-tuple-element.8) | data formatting | bytes 1048576
  36.8 0.0 copy-done
  36.8 0.7 %copy.8 = f32[16,27,128]{2,0,1:T(8,128)} copy(f32[16,27,128]{2,0,1:T(8,128)S(1)} %bitcast.3) | data formatting | bytes 442368
Async XLA Ops:
  34.9 1.9 %copy-start = (f32[27,16,128]{2,1,0:T(8,128)S(1)}, f32[27,16,128]{2,1,0:T(8,128)}, u32[]{:S(2)}) copy-start(f32[27,16,128]{2,1,0:T(8,128)} %get-tuple-element.5) | copy-start | bytes 663556
where the time goes:
time: 37.6 us; the launch traced here: 37.5 us
  Pallas kernels  34.2 us (91%)
  local copies, waits for them, and re-layouts  2.6 us (7%)
  between operations  0.65 us (2%)
    pallas_call x1, Pallas kernels, on_device(): pl.pallas_call(functools.partial(kernel, dims), out_shape=(jax.ShapeDtype...  34.2 us
    unnamed x4, local copies, waits for them, and re-layouts  2.6 us

commit v1 on v0

--- a/solution.py
+++ b/solution.py
@@ -22,8 +22,8 @@
     return [(0, 0, 2 * chunk, sizes[0]), (sizes[0] * nz, 2 * chunk, chunk, sizes[1])]
 
 
-def kernel(dims, raw_hbm, in_hbm, cot_hbm, dx_ref, wg_ref, *scratch):
-    (raw_ref, in_ref, shifted, face_out, face_in, in_t, part, recv_x, send_y, recv_y, send_z, recv_z, full, std,
+def kernel(dims, raw_hbm, in_hbm, cot_hbm, dx_ref, full, std, coef_ref, *scratch):
+    (raw_ref, in_ref, shifted, face_out, face_in, in_t, part, recv_x, send_y, recv_y, send_z, recv_z,
      std_all, w_cat, stats, stats_in, total_in, load_sem, halo_send, halo_recv, x_send, x_recv, y_send, y_recv,
      z_send, z_recv, g_send, g_recv, ay_send, ay_recv, ax_send, ax_recv, st_send, st_recv, t_send, t_recv) = scratch
     count = dict(zip(AXES, dims))
@@ -361,10 +361,27 @@
     )
     square_sum = jnp.sum(inv_std * inv_std * spread, axis=1, keepdims=True)
     scale = jnp.minimum(1.0, clip_norm * lax.rsqrt(square_sum + norm_eps))
-    factor = inv_std * scale
-    for u, t in enumerate(order):
-        value = full[slots[u]].astype(F32)
-        wg_ref[t] = factor * (value - mean_grad - std[slots[u]] * mean_cross)
+    coef_ref[0:1] = inv_std * scale
+    coef_ref[1:2] = mean_grad
+    coef_ref[2:3] = mean_cross
+
+
+def tap_slots(taps, nz):
+    order = [t for c in (1, 0, 2) for t in range(c, taps, 3)]
+    slots = [b + v for b, first, many, size in z_groups(taps, nz) for v in range(many)]
+    return list(zip(order, slots))
+
+
+def finish_kernel(nz, taps, dx_in, full, std, coef_ref, dx_hbm, wg_hbm, wg_ref, sem):
+    out_dx = pltpu.make_async_copy(dx_in, dx_hbm, sem.at[0])
+    out_dx.start()
+    factor, mean_grad, mean_cross = coef_ref[0:1], coef_ref[1:2], coef_ref[2:3]
+    for t, slot in tap_slots(taps, nz):
+        wg_ref[t] = factor * (full[slot].astype(F32) - mean_grad - std[slot] * mean_cross)
+    out_wg = pltpu.make_async_copy(wg_ref, wg_hbm, sem.at[1])
+    out_wg.start()
+    out_wg.wait()
+    out_dx.wait()
 
 
 def on_device(dims, raw_weight, inputs, cotangent):
@@ -393,8 +410,6 @@
         pltpu.VMEM((ny - 1, taps, rows, chan), BF16),
         pltpu.VMEM((padded_taps, rows, chan), BF16),
         pltpu.VMEM((nz - 1, piece, rows, chan), BF16),
-        pltpu.VMEM((padded_taps, rows, chan), BF16),
-        pltpu.VMEM((padded_taps, rows, chan), F32),
         pltpu.VMEM((nx, ny, taps, rows, chan), BF16),
         pltpu.VMEM((chan, taps * chan), BF16),
         pltpu.VMEM((2, 8, chan), F32),
@@ -405,19 +420,32 @@
     ]
     vmem = pl.BlockSpec(memory_space=pltpu.VMEM)
     anywhere = pl.BlockSpec(memory_space=pl.ANY)
+    dx, full, std, coef = pl.pallas_call(
+        functools.partial(kernel, dims),
+        out_shape=(
+            pltpu.VMEM(cotangent.shape, BF16),
+            pltpu.VMEM((padded_taps, rows, chan), BF16),
+            pltpu.VMEM((padded_taps, rows, chan), F32),
+            pltpu.VMEM((8, chan), F32),
+        ),
+        in_specs=[anywhere] * 3,
+        out_specs=(vmem,) * 4,
+        scratch_shapes=scratch,
+        compiler_params=pltpu.CompilerParams(
+            collective_id=0, has_side_effects=True, vmem_limit_bytes=40 * 1024 * 1024
+        ),
+    )(*[pltpu.with_memory_space_constraint(v, pltpu.HBM) for v in (jnp.transpose(raw_weight, (1, 0, 2)), inputs, cotangent)])
     input_grad, weight_grad = pl.pallas_call(
-        functools.partial(kernel, dims),
+        functools.partial(finish_kernel, nz, taps),
         out_shape=(
             jax.ShapeDtypeStruct(cotangent.shape, BF16),
             jax.ShapeDtypeStruct((taps, rows, chan), F32),
         ),
-        in_specs=[anywhere] * 3,
-        out_specs=(vmem, vmem),
-        scratch_shapes=scratch,
-        compiler_params=pltpu.CompilerParams(
-            collective_id=0, has_side_effects=True, vmem_limit_bytes=60 * 1024 * 1024
-        ),
-    )(jnp.transpose(raw_weight, (1, 0, 2)), inputs, cotangent)
+        in_specs=[vmem] * 4,
+        out_specs=(anywhere,) * 2,
+        scratch_shapes=[pltpu.VMEM((taps, rows, chan), F32), dma((2,))],
+        compiler_params=pltpu.CompilerParams(vmem_limit_bytes=8 * 1024 * 1024),
+    )(dx, full, std, coef)
     return input_grad, jnp.transpose(weight_grad, (1, 0, 2))
 
 

time: 37.6 us -> 35.1 us (0.934)
  local copies, waits for them, and re-layouts: 2.6 us -> 0 us
    unnamed x4 -> x0, local copies, waits for them, and re-layouts: 2.6 us -> none
    pallas_call x1 -> x2, Pallas kernels: 34.2 us -> 34.3 us  [the longest x1 33.5 us: on_device(): pl.pallas_call(functools.partial(kernel, dims), out_shape=(pltpu.VMEM(cot...]
where the time goes in v1:
time: 35.1 us; the launch traced here: 35 us
  Pallas kernels  34.3 us (98%)
  between operations  0.64 us (2%)
    pallas_call x1, Pallas kernels, on_device(): pl.pallas_call(functools.partial(kernel, dims), out_shape=(pltpu.VMEM(cot...  33.5 us
    pallas_call x1, Pallas kernels, on_device(): pl.pallas_call(functools.partial(finish_kernel, nz, taps), out_shape=(jax...  0.88 us

profile of v1, /device:TPU:0, one launch (start us, length us, event | category | flops | bytes accessed | tf_op | source)
XLA Modules:
  0.0 35.0 jit_solution(4672019241032385779)
XLA Ops:
  0.6 33.5 %shard_map.50 = (bf16[8,16,16,128]{3,2,1,0:T(8,128)(2,1)S(1)}, bf16[32,16,128]{2,1,0:T(8,128)(2,1)S(1)}, f32[32,16,128]{2,1,0:T(8,128)S(1)}, f32[8,128]{1,0:T(8,128)S(1)}) custom-call(f32[27,16,128]{2,1,0:T(8,128)} %bitcast.2, bf16[8,16,16,128]{3,2,1,0:T(8,128)(2,1)} %in_hbm.1, bf16[8,16,16,128]{3,2,1,0:T(8,128)(2,1)} %cot_hbm.1), custom_call_target="tpu_custom_call" | custom-call | tf_op jit(solution)/shard_map/pallas_call | solution.py:423
  34.1 0.9 %shard_map.51 = (bf16[8,16,16,128]{3,2,1,0:T(8,128)(2,1)}, f32[27,16,128]{2,1,0:T(8,128)}) custom-call(bf16[8,16,16,128]{3,2,1,0:T(8,128)(2,1)S(1)} %get-tuple-element.8.dx_in, bf16[32,16,128]{2,1,0:T(8,128)(2,1)S(1)} %get-tuple-element.9.full, f32[32,16,128]{2,1,0:T(8,128)S(1)} %get-tuple-element.10.std, f32[8,128]{1,0:T(8,128)S(1)} %get-tuple-element.11.coef_ref), custom_call_target="tpu_custom_call" | custom-call | tf_op jit(solution)/shard_map/pallas_call | solution.py:438

commit v2 on v1

v2 whole, which is shorter than its diff:
```python
import functools

import jax
import jax.numpy as jnp
from jax import lax
from jax.experimental import pallas as pl
from jax.experimental.pallas import tpu as pltpu
from jax.sharding import PartitionSpec as P

var_eps = 1e-05
norm_eps = 1e-06
clip_norm = 600.0
F32 = jnp.float32
BF16 = jnp.bfloat16
MESH = pl.DeviceIdType.MESH
AXES = ("gx", "gy", "gz")


def z_groups(taps, nz):
    most = nz * max(1, 8 // nz)
    groups, first, base = [], 0, 0
    while first < taps:
        many = min(most, taps - first)
        size = -(-many // nz)
        groups.append((base, first, many, size))
        first, base = first + many, base + size * nz
    return groups


def tap_slots(taps, nz):
    order = [t for c in (1, 0, 2) for t in range(c, taps, 3)]
    slots = [base + v for base, first, many, size in z_groups(taps, nz) for v in range(many)]
    return list(zip(order, slots))


def first_taps(taps):
    return taps // 3


def kernel(dims, raw_hbm, in_hbm, cot_hbm, dx_ref, full, std, coef_ref, *scratch):
    (raw_ref, in_ref, shifted, face_out, face_in, in_t, part, recv_x, send_y, recv_y, send_z, total_z, recv_z,
     std_all, w_cat, dx_part, stats, stats_in, total_in, load_sem, halo_send, halo_recv, x_send, x_recv, y_send, y_recv,
     z_send, z_recv, g_send, g_recv, ay_send, ay_recv, ax_send, ax_recv, st_send, st_recv, t_send, t_recv) = scratch
    count = dict(zip(AXES, dims))
    nx, ny, nz = dims
    me = {axis: lax.axis_index(axis) for axis in AXES}
    taps, rows, chan = raw_ref.shape
    ex, ey, ez = in_ref.shape[:3]
    groups = z_groups(taps, nz)
    order = [t for t, slot in tap_slots(taps, nz)]
    slots = [slot for t, slot in tap_slots(taps, nz)]
    early = first_taps(taps)
    fan_count = float(rows * nx * ny * taps)

    def peer(axis, k):
        return lax.rem(me[axis] + k, count[axis])

    def plane_peer(k):
        flat = lax.rem(me["gx"] * ny + me["gy"] + k, nx * ny)
        return {"gx": lax.div(flat, ny), "gy": lax.rem(flat, ny)}

    def remote(src, dst, send_sem, recv_sem, where):
        return pltpu.make_async_remote_copy(
            src_ref=src, dst_ref=dst, send_sem=send_sem, recv_sem=recv_sem,
            device_id=where, device_id_type=MESH,
        )

    def wait_all(copies):
        for copy in copies:
            copy.wait()

    def inside(step):
        within = None
        for axis, d in zip(AXES, step):
            if d:
                near = me[axis] + d
                ok = near >= 0 if d < 0 else near < count[axis]
                within = ok if within is None else jnp.logical_and(within, ok)
        return within

    def neighbour(step):
        return {axis: lax.min(lax.max(me[axis] + d, 0), count[axis] - 1) for axis, d in zip(AXES, step)}

    body = pl.ds(1, ey)
    load_cot = pltpu.make_async_copy(cot_hbm, shifted.at[1, pl.ds(1, ex), body], load_sem.at[1])
    load_raw = pltpu.make_async_copy(raw_hbm, raw_ref, load_sem.at[0])
    load_in = pltpu.make_async_copy(in_hbm, in_ref, load_sem.at[2])
    load_cot.start()
    load_raw.start()
    load_in.start()

    barrier = pltpu.get_barrier_semaphore()
    greeted = jnp.int32(nx * ny - 1 + nz - 1)
    for k in range(1, nx * ny):
        pl.semaphore_signal(barrier, inc=1, device_id=plane_peer(k), device_id_type=MESH)
    for k in range(1, nz):
        pl.semaphore_signal(barrier, inc=1, device_id={"gz": peer("gz", k)}, device_id_type=MESH)
    plane_steps = [(0, -1, 0), (0, 1, 0), (-1, -1, 0), (-1, 1, 0), (1, -1, 0), (1, 1, 0), (-1, 0, 0), (1, 0, 0)]
    depth_steps = [(dx, dy, dz) for dz in (-1, 1)
                   for dx, dy in [(0, 0), (-1, 0), (1, 0), (0, -1), (0, 1), (-1, -1), (-1, 1), (1, -1), (1, 1)]]
    for step in depth_steps:
        if step[0] or step[1]:
            near = inside(step)

            @pl.when(near)
            def _(step=step):
                pl.semaphore_signal(barrier, inc=1, device_id=neighbour(step), device_id_type=MESH)

            greeted = greeted + near.astype(jnp.int32)

    def exchange_start(slot, base, peers):
        copies = []
        for k, where in enumerate(peers):
            copy = remote(stats.at[slot], stats_in.at[base + k], st_send.at[base + k], st_recv.at[base + k], where)
            copy.start()
            copies.append(copy)
        return copies

    zero_plane = jnp.zeros((ey + 2, ez, chan), BF16)
    zero_col = jnp.zeros((ex + 2, ez, chan), BF16)
    for axis, edge, x in [("gx", 0, 0), ("gx", nx - 1, ex + 1)]:
        @pl.when(me[axis] == edge)
        def _(x=x):
            shifted[1, x] = zero_plane
            for side in range(2):
                face_in[side, x] = jnp.zeros((ey + 2, 1, chan), F32)

    for axis, edge, y in [("gy", 0, 0), ("gy", ny - 1, ey + 1)]:
        @pl.when(me[axis] == edge)
        def _(y=y):
            shifted[1, :, y] = zero_col
            for side in range(2):
                face_in[side, :, y] = jnp.zeros((ex + 2, 1, chan), F32)

    for side, edge in [(0, 0), (1, nz - 1)]:
        @pl.when(me["gz"] == edge)
        def _(side=side):
            face_in[side] = jnp.zeros((ex + 2, ey + 2, 1, chan), F32)

    for base, first, many, size in groups:
        for v in range(base + many, base + size * nz):
            send_z[v] = jnp.zeros((rows, chan), BF16)
            total_z[v] = jnp.zeros((rows, chan), F32)
            std[v] = jnp.zeros((rows, chan), F32)

    def per_output(value):
        return jnp.sum(jnp.sum(value, axis=0), axis=0, keepdims=True)

    load_raw.wait()
    raw = raw_ref[...]
    stats[0, 0] = per_output(raw)
    stats[0, 1] = per_output(raw * raw)
    stats[0, 2] = jnp.zeros((1, chan), F32)
    load_cot.wait()
    for x in range(ex):
        plane = shifted[1, x + 1, 1:ey + 1].astype(F32)
        face_out[0, x] = plane[:, 0:1, :]
        face_out[1, x] = plane[:, ez - 1:ez, :]
    pl.semaphore_wait(barrier, greeted)
    weight_sums = exchange_start(0, 0, [plane_peer(k) for k in range(1, nx * ny)])

    def halo_start(steps, base, source, target):
        copies = []
        for number, step in enumerate(steps, base):
            copy = remote(source(step), target(step), halo_send.at[number], halo_recv.at[number], neighbour(step))
            pl.when(inside(step))(copy.start)
            copies.append((step, copy))
        return copies

    def halo_wait(copies):
        for step, copy in copies:
            pl.when(inside(step))(copy.wait_send)
            pl.when(inside([-d for d in step]))(copy.wait_recv)

    def plane_source(step):
        return shifted.at[1, {-1: 1, 0: pl.ds(1, ex), 1: ex}[step[0]], {-1: 1, 0: body, 1: ey}[step[1]]]

    def plane_target(step):
        return shifted.at[1, {-1: ex + 1, 0: pl.ds(1, ex), 1: 0}[step[0]], {-1: ey + 1, 0: body, 1: 0}[step[1]]]

    def depth_source(step):
        return face_out.at[{-1: 0, 1: 1}[step[2]], {-1: pl.ds(0, 1), 0: pl.ds(0, ex), 1: pl.ds(ex - 1, 1)}[step[0]],
                           {-1: pl.ds(0, 1), 0: pl.ds(0, ey), 1: pl.ds(ey - 1, 1)}[step[1]]]

    def depth_target(step):
        return face_in.at[{-1: 1, 1: 0}[step[2]], {-1: pl.ds(ex + 1, 1), 0: pl.ds(1, ex), 1: pl.ds(0, 1)}[step[0]],
                          {-1: pl.ds(ey + 1, 1), 0: pl.ds(1, ey), 1: pl.ds(0, 1)}[step[1]]]

    plane_halo = halo_start(plane_steps, 0, plane_source, plane_target)
    depth_halo = halo_start(depth_steps, len(plane_steps), depth_source, depth_target)
    load_in.wait()
    for x in range(ex):
        in_t[:, x * ey * ez:(x + 1) * ey * ez] = in_ref[x].reshape(ey * ez, chan).T

    wait_all(weight_sums)
    sums = stats[0]
    for k in range(len(weight_sums)):
        sums = sums + stats_in[k]
    mean_out = sums[0] / fan_count
    var_out = sums[1] / fan_count - mean_out * mean_out
    inv_std = lax.rsqrt(var_out + var_eps)
    own = std_all.at[me["gx"], me["gy"]]
    for u, t in enumerate(order):
        value = (raw_ref[t] - mean_out) * inv_std
        std[slots[u]] = value
        own[u] = value.astype(BF16)

    def gather_y_start(part_number):
        span = [pl.ds(0, early), pl.ds(early, taps - early)][part_number]
        copies = []
        for k in range(1, ny):
            index = part_number * (ny - 1) + k - 1
            copy = remote(own.at[span], own.at[span], ay_send.at[index], ay_recv.at[index], {"gy": peer("gy", k)})
            copy.start()
            copies.append(copy)
        return copies

    def gather_x_start(part_number):
        span = [pl.ds(0, early), pl.ds(early, taps - early)][part_number]
        copies = []
        for k in range(1, nx):
            index = part_number * (nx - 1) + k - 1
            mine = std_all.at[me["gx"], :, span]
            copy = remote(mine, mine, ax_send.at[index], ax_recv.at[index], {"gx": peer("gx", k)})
            copy.start()
            copies.append(copy)
        return copies

    gather_y = [gather_y_start(0)]
    halo_wait(plane_halo)

    def view(t, start, planes):
        a, b, c = t // 9, (t // 3) % 3, t % 3
        block = shifted[2 - c, pl.ds(start + 2 - a, planes), 2 - b:2 - b + ey]
        return block.reshape(planes * ey * ez, chan)

    def filter_chunk(g):
        base, first, many, size = groups[g]
        for u in range(first, first + many, 2):
            group = list(range(u, min(u + 2, first + many)))
            views = [view(order[v], 0, ex) for v in group]
            right = jnp.concatenate(views, axis=1) if len(views) > 1 else views[0]
            product = jnp.dot(in_t[...], right, preferred_element_type=F32)
            for j, v in enumerate(group):
                for gx in range(nx):
                    for gy in range(ny):
                        low = (gx * ny + gy) * rows
                        part[gx, gy, v] = product[low:low + rows, j * chan:(j + 1) * chan]
        copies = []
        span = pl.ds(first, many)
        for k in range(1, nx):
            index = g * (nx - 1) + k - 1
            copy = remote(part.at[peer("gx", k), :, span], recv_x.at[k - 1, :, span],
                          x_send.at[index], x_recv.at[index], {"gx": peer("gx", k)})
            copy.start()
            copies.append(copy)
        return copies

    def rows_total(gy, span):
        total = part[me["gx"], gy, span]
        for k in range(1, nx):
            total = total + recv_x[k - 1, gy, span]
        return total

    def rows_chunk(g, copies):
        wait_all(copies)
        base, first, many, size = groups[g]
        span = pl.ds(first, many)
        for gy in range(ny):
            send_y[gy, span] = rows_total(gy, span).astype(BF16)
        sent = []
        for k in range(1, ny):
            index = g * (ny - 1) + k - 1
            copy = remote(send_y.at[peer("gy", k), span], recv_y.at[k - 1, span],
                          y_send.at[index], y_recv.at[index], {"gy": peer("gy", k)})
            copy.start()
            sent.append(copy)
        return sent

    depth_index = lax.broadcasted_iota(jnp.int32, (ey + 2, ez, chan), 1)

    def shift(slot, side, amount, edge):
        for x in range(ex + 2):
            plane = shifted[1, x].astype(F32)
            outer = face_in[side, x]
            shifted[slot, x] = jnp.where(depth_index == edge, outer, pltpu.roll(plane, amount, 1)).astype(BF16)

    reduce_x, reduce_y = [filter_chunk(0)], []
    halo_wait(depth_halo)
    shift(2, 1, ez - 1, ez - 1)
    shift(0, 0, 1, 0)
    for g in range(1, len(groups)):
        reduce_x.append(filter_chunk(g))
        reduce_y.append(rows_chunk(g - 1, reduce_x[g - 1]))
    reduce_y.append(rows_chunk(len(groups) - 1, reduce_x[-1]))
    gather_y.append(gather_y_start(1))
    wait_all(gather_y[0])
    gather_x = [gather_x_start(0)]

    step = 2 if ex % 2 == 0 else 1

    def dx_pass(low, high, last):
        for u in range(low, high):
            w_cat[:, u * chan:(u + 1) * chan] = std_all[:, :, u].reshape(nx * ny * rows, chan)

        def dx_step(n, carry):
            start = n * step
            left = jnp.concatenate([view(t, start, step) for t in order[low:high]], axis=1)
            right = w_cat[:, low * chan:high * chan]
            product = lax.dot_general(left, right, (((1,), (1,)), ((), ())), preferred_element_type=F32)
            product = product.reshape(step, ey, ez, chan)
            if last:
                dx_ref[pl.ds(start, step)] = (product + dx_part[pl.ds(start, step)]).astype(BF16)
            else:
                dx_part[pl.ds(start, step)] = product
            return carry

        lax.fori_loop(0, ex // step, dx_step, 0)

    def depth_start(g):
        wait_all(reduce_y[g])
        base, first, many, size = groups[g]
        span = pl.ds(first, many)
        total = rows_total(me["gy"], span)
        for k in range(1, ny):
            total = total + recv_y[k - 1, span].astype(F32)
        total_z[base:base + many] = total
        send_z[base:base + many] = total.astype(BF16)
        copies = []
        for k in range(1, nz):
            index = g * (nz - 1) + k - 1
            copy = remote(send_z.at[pl.ds(base + peer("gz", k) * size, size)],
                          recv_z.at[k - 1, pl.ds(base // nz, size)],
                          z_send.at[index], z_recv.at[index], {"gz": peer("gz", k)})
            copy.start()
            copies.append(copy)
        return copies

    def depth_sum(g, copies):
        wait_all(copies)
        base, first, many, size = groups[g]
        mine = pl.ds(base + me["gz"] * size, size)
        grad = total_z[mine]
        for k in range(1, nz):
            grad = grad + recv_z[k - 1, pl.ds(base // nz, size)].astype(F32)
        full[mine] = grad.astype(BF16)
        return [per_output(grad), per_output(grad * std[mine]), per_output(grad * grad)]

    def gather_start(g):
        base, first, many, size = groups[g]
        mine = pl.ds(base + me["gz"] * size, size)
        copies = []
        for k in range(1, nz):
            index = g * (nz - 1) + k - 1
            copy = remote(full.at[mine], full.at[mine], g_send.at[index], g_recv.at[index], {"gz": peer("gz", k)})
            copy.start()
            copies.append(copy)
        return copies

    wait_all(gather_x[0])
    dx_pass(0, early, False)
    reduce_z = [depth_start(g) for g in range(len(groups))]
    sums, gather_z = [None] * 3, []
    for g in range(len(groups)):
        if g == len(groups) - 2:
            wait_all(gather_y[1])
            gather_x.append(gather_x_start(1))
        new = depth_sum(g, reduce_z[g])
        sums = new if g == 0 else [a + b for a, b in zip(sums, new)]
        if g < len(groups) - 1:
            gather_z += gather_start(g)
    for n in range(3):
        stats[1, n] = sums[n]
    flat = (me["gx"] * ny + me["gy"]) * nz + me["gz"]
    total_in[flat] = stats[1]
    final_sums = []
    for k in range(1, nx * ny * nz):
        other = lax.rem(flat + k, nx * ny * nz)
        where = {
            "gx": lax.div(other, ny * nz),
            "gy": lax.rem(lax.div(other, nz), ny),
            "gz": lax.rem(other, nz),
        }
        copy = remote(stats.at[1], total_in.at[flat], t_send.at[k - 1], t_recv.at[k - 1], where)
        copy.start()
        final_sums.append(copy)
    gather_z += gather_start(len(groups) - 1)
    wait_all(gather_x[1])
    dx_pass(early, taps, True)
    wait_all(final_sums)
    sums = total_in[0]
    for k in range(1, nx * ny * nz):
        sums = sums + total_in[k]
    sum_grad, sum_cross, sum_square = sums[0], sums[1], sums[2]
    mean_grad = sum_grad / fan_count
    mean_cross = sum_cross / fan_count
    spread = sum_square - 2.0 * mean_grad * sum_grad - 2.0 * mean_cross * sum_cross
    spread = (
        spread
        + fan_count * mean_grad * mean_grad
        + fan_count * mean_cross * mean_cross * var_out / (var_out + var_eps)
    )
    square_sum = jnp.sum(inv_std * inv_std * spread, axis=1, keepdims=True)
    scale = jnp.minimum(1.0, clip_norm * lax.rsqrt(square_sum + norm_eps))
    coef_ref[0:1] = inv_std * scale
    coef_ref[1:2] = mean_grad
    coef_ref[2:3] = mean_cross
    wait_all(gather_z)


def finish_kernel(nz, taps, dx_in, full, std, coef_ref, dx_hbm, wg_hbm, wg_ref, sem):
    out_dx = pltpu.make_async_copy(dx_in, dx_hbm, sem.at[0])
    out_dx.start()
    factor, mean_grad, mean_cross = coef_ref[0:1], coef_ref[1:2], coef_ref[2:3]
    for t, slot in tap_slots(taps, nz):
        wg_ref[t] = factor * (full[slot].astype(F32) - mean_grad - std[slot] * mean_cross)
    out_wg = pltpu.make_async_copy(wg_ref, wg_hbm, sem.at[1])
    out_wg.start()
    out_wg.wait()
    out_dx.wait()


def on_device(dims, raw_weight, inputs, cotangent):
    nx, ny, nz = dims
    rows, taps, chan = raw_weight.shape
    ex, ey, ez = inputs.shape[:3]
    groups = z_groups(taps, nz)
    many = len(groups)
    piece = sum(size for base, first, number, size in groups)
    padded_taps = piece * nz
    stat_slots = nx * ny - 1
    dma = pltpu.SemaphoreType.DMA

    def pair(n):
        return [dma((max(n, 1),)), dma((max(n, 1),))]

    scratch = [
        pltpu.VMEM((taps, rows, chan), F32),
        pltpu.VMEM(inputs.shape, BF16),
        pltpu.VMEM((3, ex + 2, ey + 2, ez, chan), BF16),
        pltpu.VMEM((2, ex, ey, 1, chan), F32),
        pltpu.VMEM((2, ex + 2, ey + 2, 1, chan), F32),
        pltpu.VMEM((chan, ex * ey * ez), BF16),
        pltpu.VMEM((nx, ny, taps, rows, chan), F32),
        pltpu.VMEM((nx - 1, ny, taps, rows, chan), F32),
        pltpu.VMEM((ny, taps, rows, chan), BF16),
        pltpu.VMEM((ny - 1, taps, rows, chan), BF16),
        pltpu.VMEM((padded_taps, rows, chan), BF16),
        pltpu.VMEM((padded_taps, rows, chan), F32),
        pltpu.VMEM((nz - 1, piece, rows, chan), BF16),
        pltpu.VMEM((nx, ny, taps, rows, chan), BF16),
        pltpu.VMEM((chan, taps * chan), BF16),
        pltpu.VMEM((ex, ey, ez, chan), F32),
        pltpu.VMEM((2, 3, 1, chan), F32),
        pltpu.VMEM((stat_slots, 3, 1, chan), F32),
        pltpu.VMEM((nx * ny * nz, 3, 1, chan), F32),
        dma((3,)), *pair(26), *pair(many * (nx - 1)), *pair(many * (ny - 1)), *pair(many * (nz - 1)),
        *pair(many * (nz - 1)), *pair(2 * (ny - 1)), *pair(2 * (nx - 1)), *pair(stat_slots), *pair(nx * ny * nz - 1),
    ]
    vmem = pl.BlockSpec(memory_space=pltpu.VMEM)
    anywhere = pl.BlockSpec(memory_space=pl.ANY)
    operands = (jnp.transpose(raw_weight, (1, 0, 2)), inputs, cotangent)
    dx, full, std, coef = pl.pallas_call(
        functools.partial(kernel, dims),
        out_shape=(
            pltpu.VMEM(cotangent.shape, BF16),
            pltpu.VMEM((padded_taps, rows, chan), BF16),
            pltpu.VMEM((padded_taps, rows, chan), F32),
            pltpu.VMEM((8, chan), F32),
        ),
        in_specs=[anywhere] * 3,
        out_specs=(vmem,) * 4,
        scratch_shapes=scratch,
        compiler_params=pltpu.CompilerParams(
            collective_id=0, has_side_effects=True, vmem_limit_bytes=40 * 1024 * 1024
        ),
    )(*[pltpu.with_memory_space_constraint(v, pltpu.HBM) for v in operands])
    input_grad, weight_grad = pl.pallas_call(
        functools.partial(finish_kernel, nz, taps),
        out_shape=(
            jax.ShapeDtypeStruct(cotangent.shape, BF16),
            jax.ShapeDtypeStruct((taps, rows, chan), F32),
        ),
        in_specs=[vmem] * 4,
        out_specs=(anywhere,) * 2,
        scratch_shapes=[pltpu.VMEM((taps, rows, chan), F32), dma((2,))],
        compiler_params=pltpu.CompilerParams(vmem_limit_bytes=8 * 1024 * 1024),
    )(dx, full, std, coef)
    return input_grad, jnp.transpose(weight_grad, (1, 0, 2))


def solution(mesh):
    dims = tuple(mesh.shape[axis] for axis in AXES)
    in_specs = (P(("gx", "gy"), None, None), P("gx", "gy", "gz", None), P("gx", "gy", "gz", None))
    out_specs = (P("gx", "gy", "gz", None), P(("gx", "gy"), None, None))
    return jax.shard_map(
        functools.partial(on_device, dims), mesh=mesh, in_specs=in_specs, out_specs=out_specs, check_vma=False
    )
```

time: 35.1 us -> 31.4 us (0.89)
  Pallas kernels: 34.3 us -> 30.6 us
    pallas_call x1, Pallas kernels: 33.5 us -> 29.7 us  [on_device(): pl.pallas_call(functools.partial(kernel, dims), out_shape=(pltpu.VMEM(cot...]
where the time goes in v2:
time: 31.4 us; the launch traced here: 31.2 us
  Pallas kernels  30.6 us (97%)
  between operations  0.64 us (2%)
    pallas_call x1, Pallas kernels, on_device(): pl.pallas_call(functools.partial(kernel, dims), out_shape=(pltpu.VMEM(cot...  29.7 us
    pallas_call x1, Pallas kernels, on_device(): pl.pallas_call(functools.partial(finish_kernel, nz, taps), out_shape=(jax...  0.88 us

profile of v2, /device:TPU:0, one launch (start us, length us, event | category | flops | bytes accessed | tf_op | source)
XLA Modules:
  0.0 31.2 jit_solution(5493738487559869597)
XLA Ops:
  0.6 29.7 %shard_map.50 = (bf16[8,16,16,128]{3,2,1,0:T(8,128)(2,1)S(1)}, bf16[28,16,128]{2,1,0:T(8,128)(2,1)S(1)}, f32[28,16,128]{2,1,0:T(8,128)S(1)}, f32[8,128]{1,0:T(8,128)S(1)}) custom-call(f32[27,16,128]{2,1,0:T(8,128)} %bitcast.2, bf16[8,16,16,128]{3,2,1,0:T(8,128)(2,1)} %in_hbm.1, bf16[8,16,16,128]{3,2,1,0:T(8,128)(2,1)} %cot_hbm.1), custom_call_target="tpu_custom_call" | custom-call | tf_op jit(solution)/shard_map/pallas_call | solution.py:463
  30.4 0.9 %shard_map.51 = (bf16[8,16,16,128]{3,2,1,0:T(8,128)(2,1)}, f32[27,16,128]{2,1,0:T(8,128)}) custom-call(bf16[8,16,16,128]{3,2,1,0:T(8,128)(2,1)S(1)} %get-tuple-element.8.dx_in, bf16[28,16,128]{2,1,0:T(8,128)(2,1)S(1)} %get-tuple-element.9.full, f32[28,16,128]{2,1,0:T(8,128)S(1)} %get-tuple-element.10.std, f32[8,128]{1,0:T(8,128)S(1)} %get-tuple-element.11.coef_ref), custom_call_target="tpu_custom_call" | custom-call | tf_op jit(solution)/shard_map/pallas_call | solution.py:478

commit v3 on v2

--- a/solution.py
+++ b/solution.py
@@ -34,7 +34,7 @@
 
 
 def first_taps(taps):
-    return taps // 3
+    return 2 * (taps // 3)
 
 
 def kernel(dims, raw_hbm, in_hbm, cot_hbm, dx_ref, full, std, coef_ref, *scratch):
@@ -65,9 +65,11 @@
             device_id=where, device_id_type=MESH,
         )
 
-    def wait_all(copies):
-        for copy in copies:
-            copy.wait()
+    def arrived(ref, sem):
+        remote(ref, ref, sem, sem, plane_peer(1)).wait_recv()
+
+    def departed(ref, sem):
+        remote(ref, ref, sem, sem, plane_peer(1)).wait_send()
 
     def inside(step):
         within = None
@@ -82,39 +84,31 @@
         return {axis: lax.min(lax.max(me[axis] + d, 0), count[axis] - 1) for axis, d in zip(AXES, step)}
 
     body = pl.ds(1, ey)
+    barrier = pltpu.get_barrier_semaphore()
+    greeted = jnp.int32(nx * ny - 1 + nz - 1)
+    plane_steps = [(0, -1, 0), (0, 1, 0), (-1, -1, 0), (-1, 1, 0), (1, -1, 0), (1, 1, 0), (-1, 0, 0), (1, 0, 0)]
+    depth_steps = [(dx, dy, dz) for dz in (-1, 1)
+                   for dx, dy in [(0, 0), (-1, 0), (1, 0), (0, -1), (0, 1), (-1, -1), (-1, 1), (1, -1), (1, 1)]]
+    for step in reversed(depth_steps):
+        if step[0] or step[1]:
+            near = inside(step)
+
+            @pl.when(near)
+            def _(step=step):
+                pl.semaphore_signal(barrier, inc=1, device_id=neighbour(step), device_id_type=MESH)
+
+            greeted = greeted + near.astype(jnp.int32)
+
+    for k in range(1, nz):
+        pl.semaphore_signal(barrier, inc=1, device_id={"gz": peer("gz", k)}, device_id_type=MESH)
+    for k in range(1, nx * ny):
+        pl.semaphore_signal(barrier, inc=1, device_id=plane_peer(k), device_id_type=MESH)
     load_cot = pltpu.make_async_copy(cot_hbm, shifted.at[1, pl.ds(1, ex), body], load_sem.at[1])
     load_raw = pltpu.make_async_copy(raw_hbm, raw_ref, load_sem.at[0])
     load_in = pltpu.make_async_copy(in_hbm, in_ref, load_sem.at[2])
     load_cot.start()
     load_raw.start()
     load_in.start()
-
-    barrier = pltpu.get_barrier_semaphore()
-    greeted = jnp.int32(nx * ny - 1 + nz - 1)
-    for k in range(1, nx * ny):
-        pl.semaphore_signal(barrier, inc=1, device_id=plane_peer(k), device_id_type=MESH)
-    for k in range(1, nz):
-        pl.semaphore_signal(barrier, inc=1, device_id={"gz": peer("gz", k)}, device_id_type=MESH)
-    plane_steps = [(0, -1, 0), (0, 1, 0), (-1, -1, 0), (-1, 1, 0), (1, -1, 0), (1, 1, 0), (-1, 0, 0), (1, 0, 0)]
-    depth_steps = [(dx, dy, dz) for dz in (-1, 1)
-                   for dx, dy in [(0, 0), (-1, 0), (1, 0), (0, -1), (0, 1), (-1, -1), (-1, 1), (1, -1), (1, 1)]]
-    for step in depth_steps:
-        if step[0] or step[1]:
-            near = inside(step)
-
-            @pl.when(near)
-            def _(step=step):
-                pl.semaphore_signal(barrier, inc=1, device_id=neighbour(step), device_id_type=MESH)
-
-            greeted = greeted + near.astype(jnp.int32)
-
-    def exchange_start(slot, base, peers):
-        copies = []
-        for k, where in enumerate(peers):
-            copy = remote(stats.at[slot], stats_in.at[base + k], st_send.at[base + k], st_recv.at[base + k], where)
-            copy.start()
-            copies.append(copy)
-        return copies
 
     zero_plane = jnp.zeros((ey + 2, ez, chan), BF16)
     zero_col = jnp.zeros((ex + 2, ez, chan), BF16)
@@ -157,14 +151,23 @@
         face_out[0, x] = plane[:, 0:1, :]
         face_out[1, x] = plane[:, ez - 1:ez, :]
     pl.semaphore_wait(barrier, greeted)
-    weight_sums = exchange_start(0, 0, [plane_peer(k) for k in range(1, nx * ny)])
+    for k in range(1, nx * ny):
+        remote(stats.at[0], stats_in.at[k - 1], st_send.at[0], st_recv.at[0], plane_peer(k)).start()
+
+    odd = lax.rem(me["gy"], 2) == 1
 
     def halo_start(steps, base, source, target):
         copies = []
         for number, step in enumerate(steps, base):
-            copy = remote(source(step), target(step), halo_send.at[number], halo_recv.at[number], neighbour(step))
-            pl.when(inside(step))(copy.start)
-            copies.append((step, copy))
+            copies.append((step, remote(source(step), target(step), halo_send.at[number], halo_recv.at[number],
+                                        neighbour(step))))
+        for far in (True, False):
+            for step, copy in copies:
+                up = odd if step[1] > 0 else jnp.logical_not(odd)
+                if step[1]:
+                    pl.when(jnp.logical_and(inside(step), up if far else jnp.logical_not(up)))(copy.start)
+                elif not far:
+                    pl.when(inside(step))(copy.start)
         return copies
 
     def halo_wait(copies):
@@ -192,9 +195,9 @@
     for x in range(ex):
         in_t[:, x * ey * ez:(x + 1) * ey * ez] = in_ref[x].reshape(ey * ez, chan).T
 
-    wait_all(weight_sums)
+    arrived(stats_in, st_recv.at[0])
     sums = stats[0]
-    for k in range(len(weight_sums)):
+    for k in range(nx * ny - 1):
         sums = sums + stats_in[k]
     mean_out = sums[0] / fan_count
     var_out = sums[1] / fan_count - mean_out * mean_out
@@ -205,28 +208,23 @@
         std[slots[u]] = value
         own[u] = value.astype(BF16)
 
-    def gather_y_start(part_number):
-        span = [pl.ds(0, early), pl.ds(early, taps - early)][part_number]
-        copies = []
+    spans = [pl.ds(0, early), pl.ds(early, taps - early)]
+
+    def gather_y_start(n):
+        mine = own.at[spans[n]]
         for k in range(1, ny):
-            index = part_number * (ny - 1) + k - 1
-            copy = remote(own.at[span], own.at[span], ay_send.at[index], ay_recv.at[index], {"gy": peer("gy", k)})
-            copy.start()
-            copies.append(copy)
-        return copies
-
-    def gather_x_start(part_number):
-        span = [pl.ds(0, early), pl.ds(early, taps - early)][part_number]
-        copies = []
+            remote(mine, mine, ay_send.at[0], ay_recv.at[n], {"gy": peer("gy", k)}).start()
+
+    def gather_x_start(n):
+        arrived(std_all.at[0, pl.ds(0, ny - 1), spans[n]], ay_recv.at[n])
+        mine = std_all.at[me["gx"], :, spans[n]]
         for k in range(1, nx):
-            index = part_number * (nx - 1) + k - 1
-            mine = std_all.at[me["gx"], :, span]
-            copy = remote(mine, mine, ax_send.at[index], ax_recv.at[index], {"gx": peer("gx", k)})
-            copy.start()
-            copies.append(copy)
-        return copies
-
-    gather_y = [gather_y_start(0)]
+            remote(mine, mine, ax_send.at[0], ax_recv.at[n], {"gx": peer("gx", k)}).start()
+
+    def gather_wait(n):
+        arrived(std_all.at[pl.ds(0, nx - 1), :, spans[n]], ax_recv.at[n])
+
+    gather_y_start(0)
     halo_wait(plane_halo)
 
     def view(t, start, planes):
@@ -246,15 +244,10 @@
                     for gy in range(ny):
                         low = (gx * ny + gy) * rows
                         part[gx, gy, v] = product[low:low + rows, j * chan:(j + 1) * chan]
-        copies = []
         span = pl.ds(first, many)
         for k in range(1, nx):
-            index = g * (nx - 1) + k - 1
-            copy = remote(part.at[peer("gx", k), :, span], recv_x.at[k - 1, :, span],
-                          x_send.at[index], x_recv.at[index], {"gx": peer("gx", k)})
-            copy.start()
-            copies.append(copy)
-        return copies
+            remote(part.at[peer("gx", k), :, span], recv_x.at[k - 1, :, span], x_send.at[0], x_recv.at[g],
+                   {"gx": peer("gx", k)}).start()
 
     def rows_total(gy, span):
         total = part[me["gx"], gy, span]
@@ -262,20 +255,15 @@
             total = total + recv_x[k - 1, gy, span]
         return total
 
-    def rows_chunk(g, copies):
-        wait_all(copies)
+    def rows_chunk(g):
         base, first, many, size = groups[g]
         span = pl.ds(first, many)
+        arrived(recv_x.at[:, :, span], x_recv.at[g])
         for gy in range(ny):
             send_y[gy, span] = rows_total(gy, span).astype(BF16)
-        sent = []
         for k in range(1, ny):
-            index = g * (ny - 1) + k - 1
-            copy = remote(send_y.at[peer("gy", k), span], recv_y.at[k - 1, span],
-                          y_send.at[index], y_recv.at[index], {"gy": peer("gy", k)})
-            copy.start()
-            sent.append(copy)
-        return sent
+            remote(send_y.at[peer("gy", k), span], recv_y.at[k - 1, span], y_send.at[0], y_recv.at[g],
+                   {"gy": peer("gy", k)}).start()
 
     depth_index = lax.broadcasted_iota(jnp.int32, (ey + 2, ez, chan), 1)
 
@@ -285,17 +273,16 @@
             outer = face_in[side, x]
             shifted[slot, x] = jnp.where(depth_index == edge, outer, pltpu.roll(plane, amount, 1)).astype(BF16)
 
-    reduce_x, reduce_y = [filter_chunk(0)], []
+    filter_chunk(0)
     halo_wait(depth_halo)
     shift(2, 1, ez - 1, ez - 1)
     shift(0, 0, 1, 0)
     for g in range(1, len(groups)):
-        reduce_x.append(filter_chunk(g))
-        reduce_y.append(rows_chunk(g - 1, reduce_x[g - 1]))
-    reduce_y.append(rows_chunk(len(groups) - 1, reduce_x[-1]))
-    gather_y.append(gather_y_start(1))
-    wait_all(gather_y[0])
-    gather_x = [gather_x_start(0)]
+        filter_chunk(g)
+        rows_chunk(g - 1)
+    rows_chunk(len(groups) - 1)
+    gather_y_start(1)
+    gather_x_start(0)
 
     step = 2 if ex % 2 == 0 else 1
 
@@ -318,28 +305,22 @@
         lax.fori_loop(0, ex // step, dx_step, 0)
 
     def depth_start(g):
-        wait_all(reduce_y[g])
         base, first, many, size = groups[g]
         span = pl.ds(first, many)
+        arrived(recv_y.at[:, span], y_recv.at[g])
         total = rows_total(me["gy"], span)
         for k in range(1, ny):
             total = total + recv_y[k - 1, span].astype(F32)
         total_z[base:base + many] = total
         send_z[base:base + many] = total.astype(BF16)
-        copies = []
         for k in range(1, nz):
-            index = g * (nz - 1) + k - 1
-            copy = remote(send_z.at[pl.ds(base + peer("gz", k) * size, size)],
-                          recv_z.at[k - 1, pl.ds(base // nz, size)],
-                          z_send.at[index], z_recv.at[index], {"gz": peer("gz", k)})
-            copy.start()
-            copies.append(copy)
-        return copies
-
-    def depth_sum(g, copies):
-        wait_all(copies)
+            remote(send_z.at[pl.ds(base + peer("gz", k) * size, size)], recv_z.at[k - 1, pl.ds(base // nz, size)],
+                   z_send.at[0], z_recv.at[g], {"gz": peer("gz", k)}).start()
+
+    def depth_sum(g):
         base, first, many, size = groups[g]
         mine = pl.ds(base + me["gz"] * size, size)
+        arrived(recv_z.at[:, pl.ds(base // nz, size)], z_recv.at[g])
         grad = total_z[mine]
         for k in range(1, nz):
             grad = grad + recv_z[k - 1, pl.ds(base // nz, size)].astype(F32)
@@ -349,31 +330,25 @@
     def gather_start(g):
         base, first, many, size = groups[g]
         mine = pl.ds(base + me["gz"] * size, size)
-        copies = []
         for k in range(1, nz):
-            index = g * (nz - 1) + k - 1
-            copy = remote(full.at[mine], full.at[mine], g_send.at[index], g_recv.at[index], {"gz": peer("gz", k)})
-            copy.start()
-            copies.append(copy)
-        return copies
-
-    wait_all(gather_x[0])
+            remote(full.at[mine], full.at[mine], g_send.at[0], g_recv.at[0], {"gz": peer("gz", k)}).start()
+
+    gather_wait(0)
     dx_pass(0, early, False)
-    reduce_z = [depth_start(g) for g in range(len(groups))]
-    sums, gather_z = [None] * 3, []
+    for g in range(len(groups)):
+        depth_start(g)
+    sums = None
     for g in range(len(groups)):
         if g == len(groups) - 2:
-            wait_all(gather_y[1])
-            gather_x.append(gather_x_start(1))
-        new = depth_sum(g, reduce_z[g])
+            gather_x_start(1)
+        new = depth_sum(g)
         sums = new if g == 0 else [a + b for a, b in zip(sums, new)]
         if g < len(groups) - 1:
-            gather_z += gather_start(g)
+            gather_start(g)
     for n in range(3):
         stats[1, n] = sums[n]
     flat = (me["gx"] * ny + me["gy"]) * nz + me["gz"]
     total_in[flat] = stats[1]
-    final_sums = []
     for k in range(1, nx * ny * nz):
         other = lax.rem(flat + k, nx * ny * nz)
         where = {
@@ -381,13 +356,20 @@
             "gy": lax.rem(lax.div(other, nz), ny),
             "gz": lax.rem(other, nz),
         }
-        copy = remote(stats.at[1], total_in.at[flat], t_send.at[k - 1], t_recv.at[k - 1], where)
-        copy.start()
-        final_sums.append(copy)
-    gather_z += gather_start(len(groups) - 1)
-    wait_all(gather_x[1])
+        remote(stats.at[1], total_in.at[flat], t_send.at[0], t_recv.at[0], where).start()
+    gather_start(len(groups) - 1)
+    gather_wait(1)
     dx_pass(early, taps, True)
-    wait_all(final_sums)
+    departed(stats_in, st_send.at[0])
+    departed(part.at[pl.ds(0, nx - 1)], x_send.at[0])
+    departed(send_y.at[pl.ds(0, ny - 1)], y_send.at[0])
+    departed(recv_z, z_send.at[0])
+    departed(recv_z, g_send.at[0])
+    departed(std_all.at[0, pl.ds(0, ny - 1)], ay_send.at[0])
+    departed(std_all.at[pl.ds(0, nx - 1)], ax_send.at[0])
+    others = total_in.at[pl.ds(0, nx * ny * nz - 1)]
+    departed(others, t_send.at[0])
+    arrived(others, t_recv.at[0])
     sums = total_in[0]
     for k in range(1, nx * ny * nz):
         sums = sums + total_in[k]
@@ -405,7 +387,7 @@
     coef_ref[0:1] = inv_std * scale
     coef_ref[1:2] = mean_grad
     coef_ref[2:3] = mean_cross
-    wait_all(gather_z)
+    arrived(recv_z, g_recv.at[0])
 
 
 def finish_kernel(nz, taps, dx_in, full, std, coef_ref, dx_hbm, wg_hbm, wg_ref, sem):
@@ -431,8 +413,8 @@
     stat_slots = nx * ny - 1
     dma = pltpu.SemaphoreType.DMA
 
-    def pair(n):
-        return [dma((max(n, 1),)), dma((max(n, 1),))]
+    def pair(n, m):
+        return [dma((n,)), dma((m,))]
 
     scratch = [
         pltpu.VMEM((taps, rows, chan), F32),
@@ -454,8 +436,8 @@
         pltpu.VMEM((2, 3, 1, chan), F32),
         pltpu.VMEM((stat_slots, 3, 1, chan), F32),
         pltpu.VMEM((nx * ny * nz, 3, 1, chan), F32),
-        dma((3,)), *pair(26), *pair(many * (nx - 1)), *pair(many * (ny - 1)), *pair(many * (nz - 1)),
-        *pair(many * (nz - 1)), *pair(2 * (ny - 1)), *pair(2 * (nx - 1)), *pair(stat_slots), *pair(nx * ny * nz - 1),
+        dma((3,)), *pair(26, 26), *pair(1, many), *pair(1, many), *pair(1, many), *pair(1, 1), *pair(1, 2), *pair(1, 2),
+        *pair(1, 1), *pair(1, 1),
     ]
     vmem = pl.BlockSpec(memory_space=pltpu.VMEM)
     anywhere = pl.BlockSpec(memory_space=pl.ANY)

time: 31.4 us -> 31.3 us (level)
  no operation moved by 1% of the time
where the time goes in v3:
time: 31.3 us; the launch traced here: 31.1 us
  Pallas kernels  30.5 us (97%)
  between operations  0.64 us (2%)
    pallas_call x1, Pallas kernels, on_device(): pl.pallas_call(functools.partial(kernel, dims), out_shape=(pltpu.VMEM(cot...  29.6 us
    pallas_call x1, Pallas kernels, on_device(): pl.pallas_call(functools.partial(finish_kernel, nz, taps), out_shape=(jax...  0.88 us

profile of v3, /device:TPU:0, one launch (start us, length us, event | category | flops | bytes accessed | tf_op | source)
XLA Modules:
  0.0 31.1 jit_solution(15798047433534304801)
XLA Ops:
  0.6 29.6 %shard_map.50 = (bf16[8,16,16,128]{3,2,1,0:T(8,128)(2,1)S(1)}, bf16[28,16,128]{2,1,0:T(8,128)(2,1)S(1)}, f32[28,16,128]{2,1,0:T(8,128)S(1)}, f32[8,128]{1,0:T(8,128)S(1)}) custom-call(f32[27,16,128]{2,1,0:T(8,128)} %bitcast.2, bf16[8,16,16,128]{3,2,1,0:T(8,128)(2,1)} %in_hbm.1, bf16[8,16,16,128]{3,2,1,0:T(8,128)(2,1)} %cot_hbm.1), custom_call_target="tpu_custom_call" | custom-call | tf_op jit(solution)/shard_map/pallas_call | solution.py:445
  30.2 0.9 %shard_map.51 = (bf16[8,16,16,128]{3,2,1,0:T(8,128)(2,1)}, f32[27,16,128]{2,1,0:T(8,128)}) custom-call(bf16[8,16,16,128]{3,2,1,0:T(8,128)(2,1)S(1)} %get-tuple-element.8.dx_in, bf16[28,16,128]{2,1,0:T(8,128)(2,1)S(1)} %get-tuple-element.9.full, f32[28,16,128]{2,1,0:T(8,128)S(1)} %get-tuple-element.10.std, f32[8,128]{1,0:T(8,128)S(1)} %get-tuple-element.11.coef_ref), custom_call_target="tpu_custom_call" | custom-call | tf_op jit(solution)/shard_map/pallas_call | solution.py:460

commit v4 on v3

--- a/solution.py
+++ b/solution.py
@@ -1,4 +1,5 @@
 import functools
+import itertools
 
 import jax
 import jax.numpy as jnp
@@ -16,29 +17,31 @@
 AXES = ("gx", "gy", "gz")
 
 
-def z_groups(taps, nz):
-    most = nz * max(1, 8 // nz)
+def tap_phases():
+    phases = [[(1, 1)], [(1, 0), (1, 2)], [(0, 1), (2, 1)], [(0, 0), (2, 0), (0, 2), (2, 2)]]
+    return [[9 * a + 3 * b + c for b, c in phase for a in range(3)] for phase in phases]
+
+
+def z_groups(nz):
     groups, first, base = [], 0, 0
-    while first < taps:
-        many = min(most, taps - first)
-        size = -(-many // nz)
-        groups.append((base, first, many, size))
-        first, base = first + many, base + size * nz
+    for phase in tap_phases():
+        left = len(phase)
+        while left:
+            many = min(8, left)
+            size = -(-many // nz)
+            groups.append((base, first, many, size))
+            first, base, left = first + many, base + size * nz, left - many
     return groups
 
 
-def tap_slots(taps, nz):
-    order = [t for c in (1, 0, 2) for t in range(c, taps, 3)]
-    slots = [base + v for base, first, many, size in z_groups(taps, nz) for v in range(many)]
+def tap_slots(nz):
+    order = [t for phase in tap_phases() for t in phase]
+    slots = [base + v for base, first, many, size in z_groups(nz) for v in range(many)]
     return list(zip(order, slots))
 
 
-def first_taps(taps):
-    return 2 * (taps // 3)
-
-
 def kernel(dims, raw_hbm, in_hbm, cot_hbm, dx_ref, full, std, coef_ref, *scratch):
-    (raw_ref, in_ref, shifted, face_out, face_in, in_t, part, recv_x, send_y, recv_y, send_z, total_z, recv_z,
+    (raw_ref, in_ref, shifted, face_out, face_in, edge_out, edge_in, in_t, part, recv_x, send_y, recv_y, send_z, total_z, recv_z,
      std_all, w_cat, dx_part, stats, stats_in, total_in, load_sem, halo_send, halo_recv, x_send, x_recv, y_send, y_recv,
      z_send, z_recv, g_send, g_recv, ay_send, ay_recv, ax_send, ax_recv, st_send, st_recv, t_send, t_recv) = scratch
     count = dict(zip(AXES, dims))
@@ -46,11 +49,14 @@
     me = {axis: lax.axis_index(axis) for axis in AXES}
     taps, rows, chan = raw_ref.shape
     ex, ey, ez = in_ref.shape[:3]
-    groups = z_groups(taps, nz)
-    order = [t for t, slot in tap_slots(taps, nz)]
-    slots = [slot for t, slot in tap_slots(taps, nz)]
-    early = first_taps(taps)
+    groups = z_groups(nz)
+    order = [t for t, slot in tap_slots(nz)]
+    slots = [slot for t, slot in tap_slots(nz)]
+    early = len(tap_phases()[0]) + len(tap_phases()[1])
     fan_count = float(rows * nx * ny * taps)
+    wide = 2 if ex % 2 == 0 else 1
+    reach = wide + 2
+    planes = 2 * wide if ex % (2 * wide) == 0 else wide
 
     def peer(axis, k):
         return lax.rem(me[axis] + k, count[axis])
@@ -84,25 +90,6 @@
         return {axis: lax.min(lax.max(me[axis] + d, 0), count[axis] - 1) for axis, d in zip(AXES, step)}
 
     body = pl.ds(1, ey)
-    barrier = pltpu.get_barrier_semaphore()
-    greeted = jnp.int32(nx * ny - 1 + nz - 1)
-    plane_steps = [(0, -1, 0), (0, 1, 0), (-1, -1, 0), (-1, 1, 0), (1, -1, 0), (1, 1, 0), (-1, 0, 0), (1, 0, 0)]
-    depth_steps = [(dx, dy, dz) for dz in (-1, 1)
-                   for dx, dy in [(0, 0), (-1, 0), (1, 0), (0, -1), (0, 1), (-1, -1), (-1, 1), (1, -1), (1, 1)]]
-    for step in reversed(depth_steps):
-        if step[0] or step[1]:
-            near = inside(step)
-
-            @pl.when(near)
-            def _(step=step):
-                pl.semaphore_signal(barrier, inc=1, device_id=neighbour(step), device_id_type=MESH)
-
-            greeted = greeted + near.astype(jnp.int32)
-
-    for k in range(1, nz):
-        pl.semaphore_signal(barrier, inc=1, device_id={"gz": peer("gz", k)}, device_id_type=MESH)
-    for k in range(1, nx * ny):
-        pl.semaphore_signal(barrier, inc=1, device_id=plane_peer(k), device_id_type=MESH)
     load_cot = pltpu.make_async_copy(cot_hbm, shifted.at[1, pl.ds(1, ex), body], load_sem.at[1])
     load_raw = pltpu.make_async_copy(raw_hbm, raw_ref, load_sem.at[0])
     load_in = pltpu.make_async_copy(in_hbm, in_ref, load_sem.at[2])
@@ -110,26 +97,52 @@
     load_raw.start()
     load_in.start()
 
+    barrier = pltpu.get_barrier_semaphore()
+    greeted = jnp.int32(nx * ny - 1 + nz - 1)
+    steps = [[(dx, dy, dz) for dx in xs for dy in ys for dz in zs]
+             for xs, ys, zs in [((-1, 1), (0,), (0,)), ((0, -1, 1), (0,), (-1, 1)), ((0, -1, 1), (-1, 1), (0,)),
+                                ((0, -1, 1), (-1, 1), (-1, 1))]]
+    for step in reversed(steps[1] + steps[3]):
+        if step[0] or step[1]:
+            near = inside(step)
+
+            @pl.when(near)
+            def _(step=step):
+                pl.semaphore_signal(barrier, inc=1, device_id=neighbour(step), device_id_type=MESH)
+
+            greeted = greeted + near.astype(jnp.int32)
+
+    for k in range(1, nz):
+        pl.semaphore_signal(barrier, inc=1, device_id={"gz": peer("gz", k)}, device_id_type=MESH)
+    for k in range(1, nx * ny):
+        pl.semaphore_signal(barrier, inc=1, device_id=plane_peer(k), device_id_type=MESH)
+    for u in range(0, taps, 3):
+        for j in range(wide):
+            for p in range(reach):
+                if not 0 <= p - j <= 2:
+                    w_cat[j * chan:(j + 1) * chan, (u // 3 * reach + p) * chan:(u // 3 * reach + p + 1) * chan] = (
+                        jnp.zeros((chan, chan), BF16))
     zero_plane = jnp.zeros((ey + 2, ez, chan), BF16)
     zero_col = jnp.zeros((ex + 2, ez, chan), BF16)
     for axis, edge, x in [("gx", 0, 0), ("gx", nx - 1, ex + 1)]:
         @pl.when(me[axis] == edge)
         def _(x=x):
             shifted[1, x] = zero_plane
-            for side in range(2):
-                face_in[side, x] = jnp.zeros((ey + 2, 1, chan), F32)
-
-    for axis, edge, y in [("gy", 0, 0), ("gy", ny - 1, ey + 1)]:
+            face_in[0, x] = jnp.zeros((ey, chan), BF16)
+            face_in[1, x] = jnp.zeros((ey, chan), BF16)
+            edge_in[:, :, x] = jnp.zeros((2, 2, 1, chan), F32)
+
+    for axis, edge, y, side in [("gy", 0, 0, 0), ("gy", ny - 1, ey + 1, 1)]:
         @pl.when(me[axis] == edge)
-        def _(y=y):
+        def _(y=y, side=side):
             shifted[1, :, y] = zero_col
-            for side in range(2):
-                face_in[side, :, y] = jnp.zeros((ex + 2, 1, chan), F32)
+            edge_in[:, side] = jnp.zeros((2, ex + 2, 1, chan), F32)
 
     for side, edge in [(0, 0), (1, nz - 1)]:
         @pl.when(me["gz"] == edge)
         def _(side=side):
-            face_in[side] = jnp.zeros((ex + 2, ey + 2, 1, chan), F32)
+            face_in[side] = jnp.zeros((ex + 2, ey, chan), BF16)
+            edge_in[side] = jnp.zeros((2, ex + 2, 1, chan), F32)
 
     for base, first, many, size in groups:
         for v in range(base + many, base + size * nz):
@@ -148,66 +161,79 @@
     load_cot.wait()
     for x in range(ex):
         plane = shifted[1, x + 1, 1:ey + 1].astype(F32)
-        face_out[0, x] = plane[:, 0:1, :]
-        face_out[1, x] = plane[:, ez - 1:ez, :]
+        for side, z in [(0, 0), (1, ez - 1)]:
+            face_out[side, x] = plane[:, z, :].astype(BF16)
+            edge_out[side, 0, x] = plane[0, z:z + 1, :]
+            edge_out[side, 1, x] = plane[ey - 1, z:z + 1, :]
     pl.semaphore_wait(barrier, greeted)
     for k in range(1, nx * ny):
         remote(stats.at[0], stats_in.at[k - 1], st_send.at[0], st_recv.at[0], plane_peer(k)).start()
 
     odd = lax.rem(me["gy"], 2) == 1
 
-    def halo_start(steps, base, source, target):
-        copies = []
-        for number, step in enumerate(steps, base):
-            copies.append((step, remote(source(step), target(step), halo_send.at[number], halo_recv.at[number],
-                                        neighbour(step))))
-        for far in (True, False):
-            for step, copy in copies:
+    def own_cells(d, extent, base):
+        return {-1: pl.ds(base, 1), 0: pl.ds(base, extent), 1: pl.ds(base + extent - 1, 1)}[d]
+
+    def beyond(d, extent):
+        return {-1: pl.ds(extent + 1, 1), 0: pl.ds(1, extent), 1: pl.ds(0, 1)}[d]
+
+    def halo_copy(phase, step):
+        dx, dy, dz = step
+        side = {-1: 0, 0: None, 1: 1}
+        if phase == 1:
+            pair = face_out.at[side[dz], own_cells(dx, ex, 0)], face_in.at[1 - side[dz], beyond(dx, ex)]
+        elif phase == 3:
+            pair = (edge_out.at[side[dz], side[dy], own_cells(dx, ex, 0)],
+                    edge_in.at[1 - side[dz], 1 - side[dy], beyond(dx, ex)])
+        else:
+            pair = (shifted.at[1, own_cells(dx, ex, 1), own_cells(dy, ey, 1)],
+                    shifted.at[1, beyond(dx, ex), beyond(dy, ey)])
+        return remote(*pair, halo_send.at[phase], halo_recv.at[phase], neighbour(step))
+
+    def halo_start(phase, far):
+        for step in steps[phase]:
+            near = inside(step)
+            if far is not None:
                 up = odd if step[1] > 0 else jnp.logical_not(odd)
-                if step[1]:
-                    pl.when(jnp.logical_and(inside(step), up if far else jnp.logical_not(up)))(copy.start)
-                elif not far:
-                    pl.when(inside(step))(copy.start)
-        return copies
-
-    def halo_wait(copies):
-        for step, copy in copies:
-            pl.when(inside(step))(copy.wait_send)
-            pl.when(inside([-d for d in step]))(copy.wait_recv)
-
-    def plane_source(step):
-        return shifted.at[1, {-1: 1, 0: pl.ds(1, ex), 1: ex}[step[0]], {-1: 1, 0: body, 1: ey}[step[1]]]
-
-    def plane_target(step):
-        return shifted.at[1, {-1: ex + 1, 0: pl.ds(1, ex), 1: 0}[step[0]], {-1: ey + 1, 0: body, 1: 0}[step[1]]]
-
-    def depth_source(step):
-        return face_out.at[{-1: 0, 1: 1}[step[2]], {-1: pl.ds(0, 1), 0: pl.ds(0, ex), 1: pl.ds(ex - 1, 1)}[step[0]],
-                           {-1: pl.ds(0, 1), 0: pl.ds(0, ey), 1: pl.ds(ey - 1, 1)}[step[1]]]
-
-    def depth_target(step):
-        return face_in.at[{-1: 1, 1: 0}[step[2]], {-1: pl.ds(ex + 1, 1), 0: pl.ds(1, ex), 1: pl.ds(0, 1)}[step[0]],
-                          {-1: pl.ds(ey + 1, 1), 0: pl.ds(1, ey), 1: pl.ds(0, 1)}[step[1]]]
-
-    plane_halo = halo_start(plane_steps, 0, plane_source, plane_target)
-    depth_halo = halo_start(depth_steps, len(plane_steps), depth_source, depth_target)
+                near = jnp.logical_and(near, up if far else jnp.logical_not(up))
+            pl.when(near)(halo_copy(phase, step).start)
+
+    def neighbours(axis):
+        total = (me[axis] > 0).astype(jnp.int32) + (me[axis] < count[axis] - 1).astype(jnp.int32)
+        return [(n, total == n) for n in ([count[axis] - 1] if count[axis] < 3 else [1, 2])]
+
+    def halo_wait(phase):
+        for (i, on_x), (j, on_y), (k, on_z) in itertools.product(*[neighbours(axis) for axis in AXES]):
+            along = pl.ds(0, ex + i)
+            if phase == 0:
+                size, active, others = i, on_x, j == neighbours("gy")[0][0] and k == neighbours("gz")[0][0]
+                ref = shifted.at[1, pl.ds(0, i), body]
+            elif phase == 1:
+                size, active, others = k, jnp.logical_and(on_x, on_z), j == neighbours("gy")[0][0]
+                ref = face_in.at[pl.ds(0, k), along]
+            elif phase == 2:
+                size, active, others = j, jnp.logical_and(on_x, on_y), k == neighbours("gz")[0][0]
+                ref = shifted.at[1, along, pl.ds(0, j)]
+            else:
+                size, active, others = j * k, jnp.logical_and(on_x, jnp.logical_and(on_y, on_z)), True
+                ref = edge_in.at[pl.ds(0, k), pl.ds(0, j), along]
+            if size and others:
+                @pl.when(active)
+                def _(ref=ref):
+                    departed(ref, halo_send.at[phase])
+                    arrived(ref, halo_recv.at[phase])
+
+    halo_start(2, True)
+    halo_start(2, False)
+    halo_start(0, None)
+    halo_start(1, None)
+    halo_start(3, True)
+    halo_start(3, False)
     load_in.wait()
     for x in range(ex):
         in_t[:, x * ey * ez:(x + 1) * ey * ez] = in_ref[x].reshape(ey * ez, chan).T
 
-    arrived(stats_in, st_recv.at[0])
-    sums = stats[0]
-    for k in range(nx * ny - 1):
-        sums = sums + stats_in[k]
-    mean_out = sums[0] / fan_count
-    var_out = sums[1] / fan_count - mean_out * mean_out
-    inv_std = lax.rsqrt(var_out + var_eps)
     own = std_all.at[me["gx"], me["gy"]]
-    for u, t in enumerate(order):
-        value = (raw_ref[t] - mean_out) * inv_std
-        std[slots[u]] = value
-        own[u] = value.astype(BF16)
-
     spans = [pl.ds(0, early), pl.ds(early, taps - early)]
 
     def gather_y_start(n):
@@ -224,8 +250,6 @@
     def gather_wait(n):
         arrived(std_all.at[pl.ds(0, nx - 1), :, spans[n]], ax_recv.at[n])
 
-    gather_y_start(0)
-    halo_wait(plane_halo)
 
     def view(t, start, planes):
         a, b, c = t // 9, (t // 3) % 3, t % 3
@@ -265,44 +289,22 @@
             remote(send_y.at[peer("gy", k), span], recv_y.at[k - 1, span], y_send.at[0], y_recv.at[g],
                    {"gy": peer("gy", k)}).start()
 
-    depth_index = lax.broadcasted_iota(jnp.int32, (ey + 2, ez, chan), 1)
-
-    def shift(slot, side, amount, edge):
-        for x in range(ex + 2):
-            plane = shifted[1, x].astype(F32)
-            outer = face_in[side, x]
-            shifted[slot, x] = jnp.where(depth_index == edge, outer, pltpu.roll(plane, amount, 1)).astype(BF16)
-
-    filter_chunk(0)
-    halo_wait(depth_halo)
-    shift(2, 1, ez - 1, ez - 1)
-    shift(0, 0, 1, 0)
-    for g in range(1, len(groups)):
-        filter_chunk(g)
-        rows_chunk(g - 1)
-    rows_chunk(len(groups) - 1)
-    gather_y_start(1)
-    gather_x_start(0)
-
-    step = 2 if ex % 2 == 0 else 1
-
-    def dx_pass(low, high, last):
-        for u in range(low, high):
-            w_cat[:, u * chan:(u + 1) * chan] = std_all[:, :, u].reshape(nx * ny * rows, chan)
-
-        def dx_step(n, carry):
-            start = n * step
-            left = jnp.concatenate([view(t, start, step) for t in order[low:high]], axis=1)
-            right = w_cat[:, low * chan:high * chan]
-            product = lax.dot_general(left, right, (((1,), (1,)), ((), ())), preferred_element_type=F32)
-            product = product.reshape(step, ey, ez, chan)
-            if last:
-                dx_ref[pl.ds(start, step)] = (product + dx_part[pl.ds(start, step)]).astype(BF16)
-            else:
-                dx_part[pl.ds(start, step)] = product
-            return carry
-
-        lax.fori_loop(0, ex // step, dx_step, 0)
+    depth_index = lax.broadcasted_iota(jnp.int32, (ey, ez, chan), 1)
+    edge_index = lax.broadcasted_iota(jnp.int32, (ex + 2, ez, chan), 1)
+    turns = [(2, 1, ez - 1, ez - 1), (0, 0, 1, 0)]
+
+    def shift_faces():
+        for slot, side, amount, last in turns:
+            for x in range(ex + 2):
+                plane = pltpu.roll(shifted[1, x, 1:ey + 1].astype(F32), amount, 1)
+                outer = face_in[side, x].astype(F32)[:, None, :]
+                shifted[slot, x, 1:ey + 1] = jnp.where(depth_index == last, outer, plane).astype(BF16)
+
+    def shift_edges():
+        for slot, side, amount, last in turns:
+            for end, y in [(0, 0), (1, ey + 1)]:
+                plane = pltpu.roll(shifted[1, :, y].astype(F32), amount, 1)
+                shifted[slot, :, y] = jnp.where(edge_index == last, edge_in[side, end], plane).astype(BF16)
 
     def depth_start(g):
         base, first, many, size = groups[g]
@@ -333,13 +335,77 @@
         for k in range(1, nz):
             remote(full.at[mine], full.at[mine], g_send.at[0], g_recv.at[0], {"gz": peer("gz", k)}).start()
 
+    halo_wait(0)
+    filter_chunk(0)
+    rows_chunk(0)
+    arrived(stats_in, st_recv.at[0])
+    sums = stats[0]
+    for k in range(nx * ny - 1):
+        sums = sums + stats_in[k]
+    mean_out = sums[0] / fan_count
+    var_out = sums[1] / fan_count - mean_out * mean_out
+    inv_std = lax.rsqrt(var_out + var_eps)
+    for u, t in enumerate(order):
+        value = (raw_ref[t] - mean_out) * inv_std
+        std[slots[u]] = value
+        own[u] = value.astype(BF16)
+
+    gather_y_start(0)
+    halo_wait(1)
+    shift_faces()
+    filter_chunk(1)
+    halo_wait(2)
+    filter_chunk(2)
+    rows_chunk(1)
+    halo_wait(3)
+    shift_edges()
+    for g in range(3, len(groups)):
+        filter_chunk(g)
+        rows_chunk(g - 1)
+    rows_chunk(len(groups) - 1)
+    gather_y_start(1)
+    depth_start(0)
+    gather_x_start(0)
+
+    def dx_pass(low, high, last):
+        span = slice(low * reach * chan // 3, high * reach * chan // 3)
+        for u in range(low, high):
+            a = order[u] // 9
+            for j in range(wide):
+                at = (u // 3 * reach + j + 2 - a) * chan
+                w_cat[j * chan:(j + 1) * chan, at:at + chan] = std_all[:, :, u].reshape(nx * ny * rows, chan)
+
+        def dx_step(n, carry):
+            start = n * planes
+            left = []
+            for x in range(0, planes, wide):
+                strips = []
+                for t in order[low:high:3]:
+                    b, c = (t // 3) % 3, t % 3
+                    for p in range(reach):
+                        strips.append(shifted[2 - c, start + x + p, 2 - b:2 - b + ey].reshape(ey * ez, chan))
+                left.append(jnp.concatenate(strips, axis=1))
+            left = jnp.concatenate(left, axis=0)
+            product = lax.dot_general(left, w_cat[:, span], (((1,), (1,)), ((), ())), preferred_element_type=F32)
+            for x in range(0, planes, wide):
+                for j in range(wide):
+                    plane = product[x // wide * ey * ez:(x // wide + 1) * ey * ez, j * chan:(j + 1) * chan]
+                    plane = plane.reshape(ey, ez, chan)
+                    if last:
+                        dx_ref[start + x + j] = (plane + dx_part[start + x + j]).astype(BF16)
+                    else:
+                        dx_part[start + x + j] = plane
+            return carry
+
+        lax.fori_loop(0, ex // planes, dx_step, 0)
+
     gather_wait(0)
     dx_pass(0, early, False)
-    for g in range(len(groups)):
+    for g in range(1, len(groups)):
         depth_start(g)
     sums = None
     for g in range(len(groups)):
-        if g == len(groups) - 2:
+        if g == len(groups) - 1:
             gather_x_start(1)
         new = depth_sum(g)
         sums = new if g == 0 else [a + b for a, b in zip(sums, new)]
@@ -390,11 +456,11 @@
     arrived(recv_z, g_recv.at[0])
 
 
-def finish_kernel(nz, taps, dx_in, full, std, coef_ref, dx_hbm, wg_hbm, wg_ref, sem):
+def finish_kernel(nz, dx_in, full, std, coef_ref, dx_hbm, wg_hbm, wg_ref, sem):
     out_dx = pltpu.make_async_copy(dx_in, dx_hbm, sem.at[0])
     out_dx.start()
     factor, mean_grad, mean_cross = coef_ref[0:1], coef_ref[1:2], coef_ref[2:3]
-    for t, slot in tap_slots(taps, nz):
+    for t, slot in tap_slots(nz):
         wg_ref[t] = factor * (full[slot].astype(F32) - mean_grad - std[slot] * mean_cross)
     out_wg = pltpu.make_async_copy(wg_ref, wg_hbm, sem.at[1])
     out_wg.start()
@@ -406,7 +472,8 @@
     nx, ny, nz = dims
     rows, taps, chan = raw_weight.shape
     ex, ey, ez = inputs.shape[:3]
-    groups = z_groups(taps, nz)
+    groups = z_groups(nz)
+    wide = 2 if ex % 2 == 0 else 1
     many = len(groups)
     piece = sum(size for base, first, number, size in groups)
     padded_taps = piece * nz
@@ -420,8 +487,10 @@
         pltpu.VMEM((taps, rows, chan), F32),
         pltpu.VMEM(inputs.shape, BF16),
         pltpu.VMEM((3, ex + 2, ey + 2, ez, chan), BF16),
-        pltpu.VMEM((2, ex, ey, 1, chan), F32),
-        pltpu.VMEM((2, ex + 2, ey + 2, 1, chan), F32),
+        pltpu.VMEM((2, ex, ey, chan), BF16),
+        pltpu.VMEM((2, ex + 2, ey, chan), BF16),
+        pltpu.VMEM((2, 2, ex, 1, chan), F32),
+        pltpu.VMEM((2, 2, ex + 2, 1, chan), F32),
         pltpu.VMEM((chan, ex * ey * ez), BF16),
         pltpu.VMEM((nx, ny, taps, rows, chan), F32),
         pltpu.VMEM((nx - 1, ny, taps, rows, chan), F32),
@@ -431,12 +500,12 @@
         pltpu.VMEM((padded_taps, rows, chan), F32),
         pltpu.VMEM((nz - 1, piece, rows, chan), BF16),
         pltpu.VMEM((nx, ny, taps, rows, chan), BF16),
-        pltpu.VMEM((chan, taps * chan), BF16),
+        pltpu.VMEM((wide * chan, taps // 3 * (wide + 2) * chan), BF16),
         pltpu.VMEM((ex, ey, ez, chan), F32),
         pltpu.VMEM((2, 3, 1, chan), F32),
         pltpu.VMEM((stat_slots, 3, 1, chan), F32),
         pltpu.VMEM((nx * ny * nz, 3, 1, chan), F32),
-        dma((3,)), *pair(26, 26), *pair(1, many), *pair(1, many), *pair(1, many), *pair(1, 1), *pair(1, 2), *pair(1, 2),
+        dma((3,)), *pair(4, 4), *pair(1, many), *pair(1, many), *pair(1, many), *pair(1, 1), *pair(1, 2), *pair(1, 2),
         *pair(1, 1), *pair(1, 1),
     ]
     vmem = pl.BlockSpec(memory_space=pltpu.VMEM)
@@ -458,7 +527,7 @@
         ),
     )(*[pltpu.with_memory_space_constraint(v, pltpu.HBM) for v in operands])
     input_grad, weight_grad = pl.pallas_call(
-        functools.partial(finish_kernel, nz, taps),
+        functools.partial(finish_kernel, nz),
         out_shape=(
             jax.ShapeDtypeStruct(cotangent.shape, BF16),
             jax.ShapeDtypeStruct((taps, rows, chan), F32),

time: 31.3 us -> 29.2 us (0.933)
  Pallas kernels: 30.5 us -> 28.4 us
    pallas_call x1, Pallas kernels: 29.6 us -> 27.5 us  [on_device(): pl.pallas_call(functools.partial(kernel, dims), out_shape=(pltpu.VMEM(cot...]
where the time goes in v4:
time: 29.2 us; the launch traced here: 29 us
  Pallas kernels  28.4 us (97%)
  between operations  0.64 us (2%)
    pallas_call x1, Pallas kernels, on_device(): pl.pallas_call(functools.partial(kernel, dims), out_shape=(pltpu.VMEM(cot...  27.5 us
    pallas_call x1, Pallas kernels, on_device(): pl.pallas_call(functools.partial(finish_kernel, nz), out_shape=(jax.Shape...  0.88 us

profile of v4, /device:TPU:0, one launch (start us, length us, event | category | flops | bytes accessed | tf_op | source)
XLA Modules:
  0.0 29.0 jit_solution(16534875276560227585)
XLA Ops:
  0.6 27.5 %shard_map.50 = (bf16[8,16,16,128]{3,2,1,0:T(8,128)(2,1)S(1)}, bf16[32,16,128]{2,1,0:T(8,128)(2,1)S(1)}, f32[32,16,128]{2,1,0:T(8,128)S(1)}, f32[8,128]{1,0:T(8,128)S(1)}) custom-call(f32[27,16,128]{2,1,0:T(8,128)} %bitcast.2, bf16[8,16,16,128]{3,2,1,0:T(8,128)(2,1)} %in_hbm.1, bf16[8,16,16,128]{3,2,1,0:T(8,128)(2,1)} %cot_hbm.1), custom_call_target="tpu_custom_call" | custom-call | tf_op jit(solution)/shard_map/pallas_call | solution.py:514
  28.2 0.9 %shard_map.51 = (bf16[8,16,16,128]{3,2,1,0:T(8,128)(2,1)}, f32[27,16,128]{2,1,0:T(8,128)}) custom-call(bf16[8,16,16,128]{3,2,1,0:T(8,128)(2,1)S(1)} %get-tuple-element.8.dx_in, bf16[32,16,128]{2,1,0:T(8,128)(2,1)S(1)} %get-tuple-element.9.full, f32[32,16,128]{2,1,0:T(8,128)S(1)} %get-tuple-element.10.std, f32[8,128]{1,0:T(8,128)S(1)} %get-tuple-element.11.coef_ref), custom_call_target="tpu_custom_call" | custom-call | tf_op jit(solution)/shard_map/pallas_call | solution.py:529

commit v5 on v4

--- a/solution.py
+++ b/solution.py
@@ -17,31 +17,31 @@
 AXES = ("gx", "gy", "gz")
 
 
-def tap_phases():
-    phases = [[(1, 1)], [(1, 0), (1, 2)], [(0, 1), (2, 1)], [(0, 0), (2, 0), (0, 2), (2, 2)]]
-    return [[9 * a + 3 * b + c for b, c in phase for a in range(3)] for phase in phases]
+def tap_order():
+    pairs = [(1, 1), (1, 0), (1, 2), (0, 1), (2, 1), (0, 0), (2, 0), (0, 2), (2, 2)]
+    return [9 * a + 3 * b + c for b, c in pairs for a in range(3)]
 
 
 def z_groups(nz):
     groups, first, base = [], 0, 0
-    for phase in tap_phases():
-        left = len(phase)
-        while left:
-            many = min(8, left)
-            size = -(-many // nz)
-            groups.append((base, first, many, size))
-            first, base, left = first + many, base + size * nz, left - many
+    for many in (3, 8, 8, 4, 4):
+        size = -(-many // nz)
+        groups.append((base, first, many, size))
+        first, base = first + many, base + size * nz
     return groups
 
 
+depth_first = 1
+
+
 def tap_slots(nz):
-    order = [t for phase in tap_phases() for t in phase]
+    order = tap_order()
     slots = [base + v for base, first, many, size in z_groups(nz) for v in range(many)]
     return list(zip(order, slots))
 
 
 def kernel(dims, raw_hbm, in_hbm, cot_hbm, dx_ref, full, std, coef_ref, *scratch):
-    (raw_ref, in_ref, shifted, face_out, face_in, edge_out, edge_in, in_t, part, recv_x, send_y, recv_y, send_z, total_z, recv_z,
+    (raw_ref, in_ref, plain, shifted, in_y, in_z, face_turn, send_a, recv_a, send_b, recv_b, own_b, face_out, face_in, edge_out, edge_in, in_t, part, recv_x, send_y, recv_y, send_z, total_z, recv_z,
      std_all, w_cat, dx_part, stats, stats_in, total_in, load_sem, halo_send, halo_recv, x_send, x_recv, y_send, y_recv,
      z_send, z_recv, g_send, g_recv, ay_send, ay_recv, ax_send, ax_recv, st_send, st_recv, t_send, t_recv) = scratch
     count = dict(zip(AXES, dims))
@@ -52,7 +52,7 @@
     groups = z_groups(nz)
     order = [t for t, slot in tap_slots(nz)]
     slots = [slot for t, slot in tap_slots(nz)]
-    early = len(tap_phases()[0]) + len(tap_phases()[1])
+    parts = [(0, taps // 3), (taps // 3, 2 * (taps // 3)), (2 * (taps // 3), taps)]
     fan_count = float(rows * nx * ny * taps)
     wide = 2 if ex % 2 == 0 else 1
     reach = wide + 2
@@ -90,12 +90,14 @@
         return {axis: lax.min(lax.max(me[axis] + d, 0), count[axis] - 1) for axis, d in zip(AXES, step)}
 
     body = pl.ds(1, ey)
-    load_cot = pltpu.make_async_copy(cot_hbm, shifted.at[1, pl.ds(1, ex), body], load_sem.at[1])
+    load_cot = pltpu.make_async_copy(cot_hbm, plain.at[1, pl.ds(1, ex), body], load_sem.at[1])
+    load_more = pltpu.make_async_copy(cot_hbm, shifted.at[1, pl.ds(1, ex), body], load_sem.at[3])
     load_raw = pltpu.make_async_copy(raw_hbm, raw_ref, load_sem.at[0])
     load_in = pltpu.make_async_copy(in_hbm, in_ref, load_sem.at[2])
     load_cot.start()
     load_raw.start()
     load_in.start()
+    load_more.start()
 
     barrier = pltpu.get_barrier_semaphore()
     greeted = jnp.int32(nx * ny - 1 + nz - 1)
@@ -122,12 +124,16 @@
                 if not 0 <= p - j <= 2:
                     w_cat[j * chan:(j + 1) * chan, (u // 3 * reach + p) * chan:(u // 3 * reach + p + 1) * chan] = (
                         jnp.zeros((chan, chan), BF16))
-    zero_plane = jnp.zeros((ey + 2, ez, chan), BF16)
+    for slot in range(3):
+        plain[slot, :, 0] = jnp.zeros((ex + 2, ez, chan), BF16)
+        plain[slot, :, ey + 1] = jnp.zeros((ex + 2, ez, chan), BF16)
     zero_col = jnp.zeros((ex + 2, ez, chan), BF16)
     for axis, edge, x in [("gx", 0, 0), ("gx", nx - 1, ex + 1)]:
         @pl.when(me[axis] == edge)
         def _(x=x):
-            shifted[1, x] = zero_plane
+            plain[1, x, 1:ey + 1] = jnp.zeros((ey, ez, chan), BF16)
+            shifted[1, x, 0] = jnp.zeros((ez, chan), BF16)
+            shifted[1, x, ey + 1] = jnp.zeros((ez, chan), BF16)
             face_in[0, x] = jnp.zeros((ey, chan), BF16)
             face_in[1, x] = jnp.zeros((ey, chan), BF16)
             edge_in[:, :, x] = jnp.zeros((2, 2, 1, chan), F32)
@@ -160,7 +166,7 @@
     stats[0, 2] = jnp.zeros((1, chan), F32)
     load_cot.wait()
     for x in range(ex):
-        plane = shifted[1, x + 1, 1:ey + 1].astype(F32)
+        plane = plain[1, x + 1, 1:ey + 1].astype(F32)
         for side, z in [(0, 0), (1, ez - 1)]:
             face_out[side, x] = plane[:, z, :].astype(BF16)
             edge_out[side, 0, x] = plane[0, z:z + 1, :]
@@ -186,8 +192,9 @@
             pair = (edge_out.at[side[dz], side[dy], own_cells(dx, ex, 0)],
                     edge_in.at[1 - side[dz], 1 - side[dy], beyond(dx, ex)])
         else:
-            pair = (shifted.at[1, own_cells(dx, ex, 1), own_cells(dy, ey, 1)],
-                    shifted.at[1, beyond(dx, ex), beyond(dy, ey)])
+            land = plain if phase == 0 else shifted
+            pair = (plain.at[1, own_cells(dx, ex, 1), own_cells(dy, ey, 1)],
+                    land.at[1, beyond(dx, ex), beyond(dy, ey)])
         return remote(*pair, halo_send.at[phase], halo_recv.at[phase], neighbour(step))
 
     def halo_start(phase, far):
@@ -207,7 +214,7 @@
             along = pl.ds(0, ex + i)
             if phase == 0:
                 size, active, others = i, on_x, j == neighbours("gy")[0][0] and k == neighbours("gz")[0][0]
-                ref = shifted.at[1, pl.ds(0, i), body]
+                ref = plain.at[1, pl.ds(0, i), body]
             elif phase == 1:
                 size, active, others = k, jnp.logical_and(on_x, on_z), j == neighbours("gy")[0][0]
                 ref = face_in.at[pl.ds(0, k), along]
@@ -234,7 +241,7 @@
         in_t[:, x * ey * ez:(x + 1) * ey * ez] = in_ref[x].reshape(ey * ez, chan).T
 
     own = std_all.at[me["gx"], me["gy"]]
-    spans = [pl.ds(0, early), pl.ds(early, taps - early)]
+    spans = [pl.ds(low, high - low) for low, high in parts]
 
     def gather_y_start(n):
         mine = own.at[spans[n]]
@@ -251,23 +258,46 @@
         arrived(std_all.at[pl.ds(0, nx - 1), :, spans[n]], ax_recv.at[n])
 
 
-    def view(t, start, planes):
+    def view(t):
         a, b, c = t // 9, (t // 3) % 3, t % 3
-        block = shifted[2 - c, pl.ds(start + 2 - a, planes), 2 - b:2 - b + ey]
-        return block.reshape(planes * ey * ez, chan)
-
-    def filter_chunk(g):
-        base, first, many, size = groups[g]
-        for u in range(first, first + many, 2):
-            group = list(range(u, min(u + 2, first + many)))
-            views = [view(order[v], 0, ex) for v in group]
+        return plain[2 - c, 2 - a:2 - a + ex, 2 - b:2 - b + ey].reshape(ex * ey * ez, chan)
+
+    def blocks():
+        return [(gx, gy, (gx * ny + gy) * rows) for gx in range(nx) for gy in range(ny)]
+
+    def interior(first, last):
+        for u in range(first, last, 2):
+            group = list(range(u, min(u + 2, last)))
+            views = [view(order[v]) for v in group]
             right = jnp.concatenate(views, axis=1) if len(views) > 1 else views[0]
             product = jnp.dot(in_t[...], right, preferred_element_type=F32)
             for j, v in enumerate(group):
-                for gx in range(nx):
-                    for gy in range(ny):
-                        low = (gx * ny + gy) * rows
-                        part[gx, gy, v] = product[low:low + rows, j * chan:(j + 1) * chan]
+                for gx, gy, low in blocks():
+                    part[gx, gy, v] = product[low:low + rows, j * chan:(j + 1) * chan]
+
+    def correct(triple):
+        b, c = (order[3 * triple] // 3) % 3, order[3 * triple] % 3
+        left, right = [], [[] for a in range(3)]
+        if b != 1:
+            end = b // 2
+            left.append(in_y[1 - end])
+            for a in range(3):
+                right[a].append(shifted[2 - c, 2 - a:2 - a + ex, (1 - end) * (ey + 1)].reshape(ex * ez, chan))
+        if c != 1:
+            end = c // 2
+            left.append(in_z[1 - end])
+            for a in range(3):
+                face = face_in[1 - end, 2 - a:2 - a + ex] if b == 1 else face_turn[1 - end, b // 2, 2 - a:2 - a + ex]
+                right[a].append(face.reshape(ex * ey, chan))
+        left = jnp.concatenate(left, axis=1)
+        right = jnp.concatenate([jnp.concatenate(strip, axis=0) for strip in right], axis=1)
+        product = jnp.dot(left, right, preferred_element_type=F32)
+        for a in range(3):
+            for gx, gy, low in blocks():
+                part[gx, gy, 3 * triple + a] += product[low:low + rows, a * chan:(a + 1) * chan]
+
+    def rows_send(g):
+        base, first, many, size = groups[g]
         span = pl.ds(first, many)
         for k in range(1, nx):
             remote(part.at[peer("gx", k), :, span], recv_x.at[k - 1, :, span], x_send.at[0], x_recv.at[g],
@@ -283,21 +313,60 @@
         base, first, many, size = groups[g]
         span = pl.ds(first, many)
         arrived(recv_x.at[:, :, span], x_recv.at[g])
+        if g == depth_first:
+            for gy in range(ny):
+                send_a[gy, 0:many] = rows_total(gy, span).astype(BF16)
+                for v in range(many, size * nz):
+                    send_a[gy, v] = jnp.zeros((rows, chan), BF16)
+            for k in range(1, nz):
+                remote(send_a.at[:, pl.ds(peer("gz", k) * size, size)], recv_a.at[k - 1], y_send.at[1], y_recv.at[g],
+                       {"gz": peer("gz", k)}).start()
+            return
         for gy in range(ny):
             send_y[gy, span] = rows_total(gy, span).astype(BF16)
         for k in range(1, ny):
             remote(send_y.at[peer("gy", k), span], recv_y.at[k - 1, span], y_send.at[0], y_recv.at[g],
                    {"gy": peer("gy", k)}).start()
 
+    def depth_middle():
+        g = depth_first
+        base, first, many, size = groups[g]
+        arrived(recv_a, y_recv.at[g])
+        mine = pl.ds(me["gz"] * size, size)
+        for gy in range(ny):
+            total = send_a[gy, mine].astype(F32)
+            for k in range(1, nz):
+                total = total + recv_a[k - 1, gy].astype(F32)
+            own_b[gy] = total
+            send_b[gy] = total.astype(BF16)
+        for k in range(1, ny):
+            remote(send_b.at[peer("gy", k)], recv_b.at[k - 1], z_send.at[1], z_recv.at[g], {"gy": peer("gy", k)}).start()
+
     depth_index = lax.broadcasted_iota(jnp.int32, (ey, ez, chan), 1)
     edge_index = lax.broadcasted_iota(jnp.int32, (ex + 2, ez, chan), 1)
+    row_index = lax.broadcasted_iota(jnp.int32, (ex + 2, ey, chan), 1)
     turns = [(2, 1, ez - 1, ez - 1), (0, 0, 1, 0)]
 
+    def turn_plain(xs):
+        for x in xs:
+            value = plain[1, x, 1:ey + 1].astype(F32)
+            for slot, side, amount, last in turns:
+                plane = pltpu.roll(value, amount, 1)
+                plain[slot, x, 1:ey + 1] = jnp.where(depth_index == last, 0.0, plane).astype(BF16)
+
+    def turn_faces():
+        for side in range(2):
+            face = face_in[side].astype(F32)
+            for n, amount, last in [(0, ey - 1, ey - 1), (1, 1, 0)]:
+                face_turn[side, n] = jnp.where(row_index == last, 0.0, pltpu.roll(face, amount, 1)).astype(BF16)
+
     def shift_faces():
+        for x in (0, ex + 1):
+            shifted[1, x, 1:ey + 1] = plain[1, x, 1:ey + 1]
         for slot, side, amount, last in turns:
             for x in range(ex + 2):
-                plane = pltpu.roll(shifted[1, x, 1:ey + 1].astype(F32), amount, 1)
                 outer = face_in[side, x].astype(F32)[:, None, :]
+                plane = plain[slot, x, 1:ey + 1].astype(F32)
                 shifted[slot, x, 1:ey + 1] = jnp.where(depth_index == last, outer, plane).astype(BF16)
 
     def shift_edges():
@@ -322,10 +391,16 @@
     def depth_sum(g):
         base, first, many, size = groups[g]
         mine = pl.ds(base + me["gz"] * size, size)
-        arrived(recv_z.at[:, pl.ds(base // nz, size)], z_recv.at[g])
-        grad = total_z[mine]
-        for k in range(1, nz):
-            grad = grad + recv_z[k - 1, pl.ds(base // nz, size)].astype(F32)
+        if g == depth_first:
+            arrived(recv_b, z_recv.at[g])
+            grad = own_b[me["gy"]]
+            for k in range(1, ny):
+                grad = grad + recv_b[k - 1].astype(F32)
+        else:
+            arrived(recv_z.at[:, pl.ds(base // nz, size)], z_recv.at[g])
+            grad = total_z[mine]
+            for k in range(1, nz):
+                grad = grad + recv_z[k - 1, pl.ds(base // nz, size)].astype(F32)
         full[mine] = grad.astype(BF16)
         return [per_output(grad), per_output(grad * std[mine]), per_output(grad * grad)]
 
@@ -335,8 +410,15 @@
         for k in range(1, nz):
             remote(full.at[mine], full.at[mine], g_send.at[0], g_recv.at[0], {"gz": peer("gz", k)}).start()
 
+    turn_plain(range(1, ex + 1))
+    for end, y, z in [(0, 0, 0), (1, ey - 1, ez - 1)]:
+        in_y[end] = in_ref[:, y].reshape(ex * ez, chan).T
+        in_z[end] = jnp.concatenate([in_ref[x].astype(F32)[:, z, :] for x in range(ex)], axis=0).astype(BF16).T
     halo_wait(0)
-    filter_chunk(0)
+    interior(0, 3)
+    rows_send(0)
+    turn_plain((0, ex + 1))
+    interior(3, taps)
     rows_chunk(0)
     arrived(stats_in, st_recv.at[0])
     sums = stats[0]
@@ -349,25 +431,29 @@
         value = (raw_ref[t] - mean_out) * inv_std
         std[slots[u]] = value
         own[u] = value.astype(BF16)
-
     gather_y_start(0)
     halo_wait(1)
-    shift_faces()
-    filter_chunk(1)
+    turn_faces()
     halo_wait(2)
-    filter_chunk(2)
-    rows_chunk(1)
+    load_more.wait()
     halo_wait(3)
     shift_edges()
-    for g in range(3, len(groups)):
-        filter_chunk(g)
-        rows_chunk(g - 1)
-    rows_chunk(len(groups) - 1)
+    done = 3
+    for g in range(1, len(groups)):
+        base, first, many, size = groups[g]
+        while done < first + many:
+            correct(done // 3)
+            done += 3
+        rows_send(g)
+    for g in range(1, len(groups)):
+        rows_chunk(g)
     gather_y_start(1)
     depth_start(0)
     gather_x_start(0)
-
-    def dx_pass(low, high, last):
+    shift_faces()
+
+    def dx_pass(n):
+        low, high = parts[n]
         span = slice(low * reach * chan // 3, high * reach * chan // 3)
         for u in range(low, high):
             a = order[u] // 9
@@ -375,8 +461,8 @@
                 at = (u // 3 * reach + j + 2 - a) * chan
                 w_cat[j * chan:(j + 1) * chan, at:at + chan] = std_all[:, :, u].reshape(nx * ny * rows, chan)
 
-        def dx_step(n, carry):
-            start = n * planes
+        def dx_step(m, carry):
+            start = m * planes
             left = []
             for x in range(0, planes, wide):
                 strips = []
@@ -391,8 +477,10 @@
                 for j in range(wide):
                     plane = product[x // wide * ey * ez:(x // wide + 1) * ey * ez, j * chan:(j + 1) * chan]
                     plane = plane.reshape(ey, ez, chan)
-                    if last:
-                        dx_ref[start + x + j] = (plane + dx_part[start + x + j]).astype(BF16)
+                    if n > 0:
+                        plane = plane + dx_part[start + x + j]
+                    if n == len(parts) - 1:
+                        dx_ref[start + x + j] = plane.astype(BF16)
                     else:
                         dx_part[start + x + j] = plane
             return carry
@@ -400,16 +488,22 @@
         lax.fori_loop(0, ex // planes, dx_step, 0)
 
     gather_wait(0)
-    dx_pass(0, early, False)
+    dx_pass(0)
     for g in range(1, len(groups)):
-        depth_start(g)
+        if g == 3:
+            depth_middle()
+            gather_y_start(2)
+        if g != depth_first:
+            depth_start(g)
+    late = [g for g in range(len(groups)) if g != depth_first]
+    late.insert(len(late) - 1, depth_first)
     sums = None
-    for g in range(len(groups)):
-        if g == len(groups) - 1:
+    for g in late:
+        if g == late[-1]:
             gather_x_start(1)
         new = depth_sum(g)
-        sums = new if g == 0 else [a + b for a, b in zip(sums, new)]
-        if g < len(groups) - 1:
+        sums = new if sums is None else [a + b for a, b in zip(sums, new)]
+        if g != late[-1]:
             gather_start(g)
     for n in range(3):
         stats[1, n] = sums[n]
@@ -423,13 +517,19 @@
             "gz": lax.rem(other, nz),
         }
         remote(stats.at[1], total_in.at[flat], t_send.at[0], t_recv.at[0], where).start()
-    gather_start(len(groups) - 1)
+    gather_start(late[-1])
     gather_wait(1)
-    dx_pass(early, taps, True)
+    dx_pass(1)
+    gather_x_start(2)
+    gather_wait(2)
+    dx_pass(2)
     departed(stats_in, st_send.at[0])
     departed(part.at[pl.ds(0, nx - 1)], x_send.at[0])
-    departed(send_y.at[pl.ds(0, ny - 1)], y_send.at[0])
-    departed(recv_z, z_send.at[0])
+    base, first, many, size = groups[depth_first]
+    departed(recv_a, y_send.at[1])
+    departed(recv_b, z_send.at[1])
+    departed(send_y.at[pl.ds(0, ny - 1), pl.ds(0, taps - many)], y_send.at[0])
+    departed(recv_z.at[:, pl.ds(0, recv_z.shape[1] - size)], z_send.at[0])
     departed(recv_z, g_send.at[0])
     departed(std_all.at[0, pl.ds(0, ny - 1)], ay_send.at[0])
     departed(std_all.at[pl.ds(0, nx - 1)], ax_send.at[0])
@@ -477,6 +577,7 @@
     many = len(groups)
     piece = sum(size for base, first, number, size in groups)
     padded_taps = piece * nz
+    alone = groups[depth_first][3]
     stat_slots = nx * ny - 1
     dma = pltpu.SemaphoreType.DMA
 
@@ -487,6 +588,15 @@
         pltpu.VMEM((taps, rows, chan), F32),
         pltpu.VMEM(inputs.shape, BF16),
         pltpu.VMEM((3, ex + 2, ey + 2, ez, chan), BF16),
+        pltpu.VMEM((3, ex + 2, ey + 2, ez, chan), BF16),
+        pltpu.VMEM((2, chan, ex * ez), BF16),
+        pltpu.VMEM((2, chan, ex * ey), BF16),
+        pltpu.VMEM((2, 2, ex + 2, ey, chan), BF16),
+        pltpu.VMEM((ny, alone * nz, rows, chan), BF16),
+        pltpu.VMEM((nz - 1, ny, alone, rows, chan), BF16),
+        pltpu.VMEM((ny, alone, rows, chan), BF16),
+        pltpu.VMEM((ny - 1, alone, rows, chan), BF16),
+        pltpu.VMEM((ny, alone, rows, chan), F32),
         pltpu.VMEM((2, ex, ey, chan), BF16),
         pltpu.VMEM((2, ex + 2, ey, chan), BF16),
         pltpu.VMEM((2, 2, ex, 1, chan), F32),
@@ -505,7 +615,7 @@
         pltpu.VMEM((2, 3, 1, chan), F32),
         pltpu.VMEM((stat_slots, 3, 1, chan), F32),
         pltpu.VMEM((nx * ny * nz, 3, 1, chan), F32),
-        dma((3,)), *pair(4, 4), *pair(1, many), *pair(1, many), *pair(1, many), *pair(1, 1), *pair(1, 2), *pair(1, 2),
+        dma((4,)), *pair(4, 4), *pair(1, many), *pair(2, many), *pair(2, many), *pair(1, 1), *pair(1, 3), *pair(1, 3),
         *pair(1, 1), *pair(1, 1),
     ]
     vmem = pl.BlockSpec(memory_space=pltpu.VMEM)

time: 29.2 us -> 27.4 us (0.938)
  Pallas kernels: 28.4 us -> 26.6 us
    pallas_call x1, Pallas kernels: 27.5 us -> 25.7 us  [on_device(): pl.pallas_call(functools.partial(kernel, dims), out_shape=(pltpu.VMEM(cot...]
where the time goes in v5:
time: 27.4 us; the launch traced here: 27.2 us
  Pallas kernels  26.6 us (97%)
  between operations  0.64 us (2%)
    pallas_call x1, Pallas kernels, on_device(): pl.pallas_call(functools.partial(kernel, dims), out_shape=(pltpu.VMEM(cot...  25.7 us
    pallas_call x1, Pallas kernels, on_device(): pl.pallas_call(functools.partial(finish_kernel, nz), out_shape=(jax.Shape...  0.88 us

profile of v5, /device:TPU:0, one launch (start us, length us, event | category | flops | bytes accessed | tf_op | source)
XLA Modules:
  0.0 27.2 jit_solution(12441489905984258530)
XLA Ops:
  0.6 25.7 %shard_map.50 = (bf16[8,16,16,128]{3,2,1,0:T(8,128)(2,1)S(1)}, bf16[28,16,128]{2,1,0:T(8,128)(2,1)S(1)}, f32[28,16,128]{2,1,0:T(8,128)S(1)}, f32[8,128]{1,0:T(8,128)S(1)}) custom-call(f32[27,16,128]{2,1,0:T(8,128)} %bitcast.2, bf16[8,16,16,128]{3,2,1,0:T(8,128)(2,1)} %in_hbm.1, bf16[8,16,16,128]{3,2,1,0:T(8,128)(2,1)} %cot_hbm.1), custom_call_target="tpu_custom_call" | custom-call | tf_op jit(solution)/shard_map/pallas_call | solution.py:624
  26.3 0.9 %shard_map.51 = (bf16[8,16,16,128]{3,2,1,0:T(8,128)(2,1)}, f32[27,16,128]{2,1,0:T(8,128)}) custom-call(bf16[8,16,16,128]{3,2,1,0:T(8,128)(2,1)S(1)} %get-tuple-element.8.dx_in, bf16[28,16,128]{2,1,0:T(8,128)(2,1)S(1)} %get-tuple-element.9.full, f32[28,16,128]{2,1,0:T(8,128)S(1)} %get-tuple-element.10.std, f32[8,128]{1,0:T(8,128)S(1)} %get-tuple-element.11.coef_ref), custom_call_target="tpu_custom_call" | custom-call | tf_op jit(solution)/shard_map/pallas_call | solution.py:639

commit v6 on v5

--- a/solution.py
+++ b/solution.py
@@ -24,14 +24,14 @@
 
 def z_groups(nz):
     groups, first, base = [], 0, 0
-    for many in (3, 8, 8, 4, 4):
+    for many in (3, 6, 8, 6, 4):
         size = -(-many // nz)
         groups.append((base, first, many, size))
         first, base = first + many, base + size * nz
     return groups
 
 
-depth_first = 1
+depth_first = 2
 
 
 def tap_slots(nz):
@@ -41,7 +41,7 @@
 
 
 def kernel(dims, raw_hbm, in_hbm, cot_hbm, dx_ref, full, std, coef_ref, *scratch):
-    (raw_ref, in_ref, plain, shifted, in_y, in_z, face_turn, send_a, recv_a, send_b, recv_b, own_b, face_out, face_in, edge_out, edge_in, in_t, part, recv_x, send_y, recv_y, send_z, total_z, recv_z,
+    (raw_ref, in_ref, plain, shifted, in_y, in_z, face_turn, send_a, recv_a, send_b, recv_b, own_b, face_out, face_in, edge_out, edge_in, in_t, part, part_x, recv_x, send_y, recv_y, send_z, total_z, recv_z,
      std_all, w_cat, dx_part, stats, stats_in, total_in, load_sem, halo_send, halo_recv, x_send, x_recv, y_send, y_recv,
      z_send, z_recv, g_send, g_recv, ay_send, ay_recv, ax_send, ax_recv, st_send, st_recv, t_send, t_recv) = scratch
     count = dict(zip(AXES, dims))
@@ -52,14 +52,16 @@
     groups = z_groups(nz)
     order = [t for t, slot in tap_slots(nz)]
     slots = [slot for t, slot in tap_slots(nz)]
-    parts = [(0, taps // 3), (taps // 3, 2 * (taps // 3)), (2 * (taps // 3), taps)]
+    parts = [(0, 6), (6, 15), (15, taps)]
     fan_count = float(rows * nx * ny * taps)
     wide = 2 if ex % 2 == 0 else 1
     reach = wide + 2
     planes = 2 * wide if ex % (2 * wide) == 0 else wide
 
+    turned = {axis: [lax.rem(me[axis] + k, count[axis]) for k in range(count[axis])] for axis in AXES}
+
     def peer(axis, k):
-        return lax.rem(me[axis] + k, count[axis])
+        return turned[axis][k]
 
     def plane_peer(k):
         flat = lax.rem(me["gx"] * ny + me["gy"] + k, nx * ny)
@@ -273,7 +275,10 @@
             product = jnp.dot(in_t[...], right, preferred_element_type=F32)
             for j, v in enumerate(group):
                 for gx, gy, low in blocks():
-                    part[gx, gy, v] = product[low:low + rows, j * chan:(j + 1) * chan]
+                    value = product[low:low + rows, j * chan:(j + 1) * chan]
+                    part[gx, gy, v] = value
+                    if v < 3:
+                        part_x[gx, gy, v] = value.astype(BF16)
 
     def correct(triple):
         b, c = (order[3 * triple] // 3) % 3, order[3 * triple] % 3
@@ -291,22 +296,28 @@
                 right[a].append(face.reshape(ex * ey, chan))
         left = jnp.concatenate(left, axis=1)
         right = jnp.concatenate([jnp.concatenate(strip, axis=0) for strip in right], axis=1)
-        product = jnp.dot(left, right, preferred_element_type=F32)
-        for a in range(3):
-            for gx, gy, low in blocks():
-                part[gx, gy, 3 * triple + a] += product[low:low + rows, a * chan:(a + 1) * chan]
+        return jnp.dot(left, right, preferred_element_type=F32)
+
+    def correct_all(triples):
+        products = [correct(triple) for triple in triples]
+        for triple, product in zip(triples, products):
+            for a in range(3):
+                for gx, gy, low in blocks():
+                    value = part[gx, gy, 3 * triple + a] + product[low:low + rows, a * chan:(a + 1) * chan]
+                    part[gx, gy, 3 * triple + a] = value
+                    part_x[gx, gy, 3 * triple + a] = value.astype(BF16)
 
     def rows_send(g):
         base, first, many, size = groups[g]
         span = pl.ds(first, many)
         for k in range(1, nx):
-            remote(part.at[peer("gx", k), :, span], recv_x.at[k - 1, :, span], x_send.at[0], x_recv.at[g],
+            remote(part_x.at[peer("gx", k), :, span], recv_x.at[k - 1, :, span], x_send.at[0], x_recv.at[g],
                    {"gx": peer("gx", k)}).start()
 
     def rows_total(gy, span):
         total = part[me["gx"], gy, span]
         for k in range(1, nx):
-            total = total + recv_x[k - 1, gy, span]
+            total = total + recv_x[k - 1, gy, span].astype(F32)
         return total
 
     def rows_chunk(g):
@@ -420,6 +431,10 @@
     turn_plain((0, ex + 1))
     interior(3, taps)
     rows_chunk(0)
+    halo_wait(1)
+    turn_faces()
+    correct_all(range(1, 3))
+    rows_send(1)
     arrived(stats_in, st_recv.at[0])
     sums = stats[0]
     for k in range(nx * ny - 1):
@@ -432,24 +447,19 @@
         std[slots[u]] = value
         own[u] = value.astype(BF16)
     gather_y_start(0)
-    halo_wait(1)
-    turn_faces()
     halo_wait(2)
-    load_more.wait()
+    correct_all(range(3, 5))
     halo_wait(3)
     shift_edges()
-    done = 3
-    for g in range(1, len(groups)):
-        base, first, many, size = groups[g]
-        while done < first + many:
-            correct(done // 3)
-            done += 3
+    correct_all(range(5, 9))
+    for g in range(2, len(groups)):
         rows_send(g)
     for g in range(1, len(groups)):
         rows_chunk(g)
     gather_y_start(1)
     depth_start(0)
     gather_x_start(0)
+    load_more.wait()
     shift_faces()
 
     def dx_pass(n):
@@ -490,18 +500,17 @@
     gather_wait(0)
     dx_pass(0)
     for g in range(1, len(groups)):
-        if g == 3:
-            depth_middle()
-            gather_y_start(2)
         if g != depth_first:
             depth_start(g)
+    depth_middle()
+    gather_y_start(2)
     late = [g for g in range(len(groups)) if g != depth_first]
-    late.insert(len(late) - 1, depth_first)
+    late.append(depth_first)
     sums = None
     for g in late:
-        if g == late[-1]:
+        new = depth_sum(g)
+        if g == 1:
             gather_x_start(1)
-        new = depth_sum(g)
         sums = new if sums is None else [a + b for a, b in zip(sums, new)]
         if g != late[-1]:
             gather_start(g)
@@ -509,22 +518,20 @@
         stats[1, n] = sums[n]
     flat = (me["gx"] * ny + me["gy"]) * nz + me["gz"]
     total_in[flat] = stats[1]
-    for k in range(1, nx * ny * nz):
-        other = lax.rem(flat + k, nx * ny * nz)
-        where = {
-            "gx": lax.div(other, ny * nz),
-            "gy": lax.rem(lax.div(other, nz), ny),
-            "gz": lax.rem(other, nz),
-        }
-        remote(stats.at[1], total_in.at[flat], t_send.at[0], t_recv.at[0], where).start()
+    for dz in sorted(range(nz), key=lambda k: -min(k, nz - k)):
+        for dx in range(nx):
+            for dy in range(ny):
+                if dx or dy or dz:
+                    where = {"gx": peer("gx", dx), "gy": peer("gy", dy), "gz": peer("gz", dz)}
+                    remote(stats.at[1], total_in.at[flat], t_send.at[0], t_recv.at[0], where).start()
     gather_start(late[-1])
+    gather_x_start(2)
     gather_wait(1)
     dx_pass(1)
-    gather_x_start(2)
     gather_wait(2)
     dx_pass(2)
     departed(stats_in, st_send.at[0])
-    departed(part.at[pl.ds(0, nx - 1)], x_send.at[0])
+    departed(part_x.at[pl.ds(0, nx - 1)], x_send.at[0])
     base, first, many, size = groups[depth_first]
     departed(recv_a, y_send.at[1])
     departed(recv_b, z_send.at[1])
@@ -603,7 +610,8 @@
         pltpu.VMEM((2, 2, ex + 2, 1, chan), F32),
         pltpu.VMEM((chan, ex * ey * ez), BF16),
         pltpu.VMEM((nx, ny, taps, rows, chan), F32),
-        pltpu.VMEM((nx - 1, ny, taps, rows, chan), F32),
+        pltpu.VMEM((nx, ny, taps, rows, chan), BF16),
+        pltpu.VMEM((nx - 1, ny, taps, rows, chan), BF16),
         pltpu.VMEM((ny, taps, rows, chan), BF16),
         pltpu.VMEM((ny - 1, taps, rows, chan), BF16),
         pltpu.VMEM((padded_taps, rows, chan), BF16),

time: 27.4 us -> 26.8 us (0.978)
  Pallas kernels: 26.6 us -> 26 us
    pallas_call x1, Pallas kernels: 25.7 us -> 25.1 us  [on_device(): pl.pallas_call(functools.partial(kernel, dims), out_shape=(pltpu.VMEM(cot...]
where the time goes in v6:
time: 26.8 us; the launch traced here: 26.6 us
  Pallas kernels  26 us (97%)
  between operations  0.64 us (2%)
    pallas_call x1, Pallas kernels, on_device(): pl.pallas_call(functools.partial(kernel, dims), out_shape=(pltpu.VMEM(cot...  25.1 us
    pallas_call x1, Pallas kernels, on_device(): pl.pallas_call(functools.partial(finish_kernel, nz), out_shape=(jax.Shape...  0.88 us

profile of v6, /device:TPU:0, one launch (start us, length us, event | category | flops | bytes accessed | tf_op | source)
XLA Modules:
  0.0 26.6 jit_solution(13222599158783520074)
XLA Ops:
  0.6 25.1 %shard_map.50 = (bf16[8,16,16,128]{3,2,1,0:T(8,128)(2,1)S(1)}, bf16[32,16,128]{2,1,0:T(8,128)(2,1)S(1)}, f32[32,16,128]{2,1,0:T(8,128)S(1)}, f32[8,128]{1,0:T(8,128)S(1)}) custom-call(f32[27,16,128]{2,1,0:T(8,128)} %bitcast.2, bf16[8,16,16,128]{3,2,1,0:T(8,128)(2,1)} %in_hbm.1, bf16[8,16,16,128]{3,2,1,0:T(8,128)(2,1)} %cot_hbm.1), custom_call_target="tpu_custom_call" | custom-call | tf_op jit(solution)/shard_map/pallas_call | solution.py:632
  25.7 0.9 %shard_map.51 = (bf16[8,16,16,128]{3,2,1,0:T(8,128)(2,1)}, f32[27,16,128]{2,1,0:T(8,128)}) custom-call(bf16[8,16,16,128]{3,2,1,0:T(8,128)(2,1)S(1)} %get-tuple-element.8.dx_in, bf16[32,16,128]{2,1,0:T(8,128)(2,1)S(1)} %get-tuple-element.9.full, f32[32,16,128]{2,1,0:T(8,128)S(1)} %get-tuple-element.10.std, f32[8,128]{1,0:T(8,128)S(1)} %get-tuple-element.11.coef_ref), custom_call_target="tpu_custom_call" | custom-call | tf_op jit(solution)/shard_map/pallas_call | solution.py:647

commit v7 on v6

--- a/solution.py
+++ b/solution.py
@@ -52,7 +52,7 @@
     groups = z_groups(nz)
     order = [t for t, slot in tap_slots(nz)]
     slots = [slot for t, slot in tap_slots(nz)]
-    parts = [(0, 6), (6, 15), (15, taps)]
+    parts = [(0, 6), (6, 18), (18, taps)]
     fan_count = float(rows * nx * ny * taps)
     wide = 2 if ex % 2 == 0 else 1
     reach = wide + 2
@@ -353,6 +353,15 @@
         for k in range(1, ny):
             remote(send_b.at[peer("gy", k)], recv_b.at[k - 1], z_send.at[1], z_recv.at[g], {"gy": peer("gy", k)}).start()
 
+    def middle_sums():
+        base, first, many, size = groups[depth_first]
+        mine_std = pl.ds(first + me["gz"] * size, size)
+        plain_sum, cross_sum = 0.0, 0.0
+        for gy in range(ny):
+            plain_sum = plain_sum + own_b[gy]
+            cross_sum = cross_sum + own_b[gy] * std_all[me["gx"], gy, mine_std].astype(F32)
+        return [per_output(plain_sum), per_output(cross_sum)]
+
     depth_index = lax.broadcasted_iota(jnp.int32, (ey, ez, chan), 1)
     edge_index = lax.broadcasted_iota(jnp.int32, (ex + 2, ez, chan), 1)
     row_index = lax.broadcasted_iota(jnp.int32, (ex + 2, ey, chan), 1)
@@ -398,6 +407,7 @@
         for k in range(1, nz):
             remote(send_z.at[pl.ds(base + peer("gz", k) * size, size)], recv_z.at[k - 1, pl.ds(base // nz, size)],
                    z_send.at[0], z_recv.at[g], {"gz": peer("gz", k)}).start()
+        return [per_output(total), per_output(total * std[base:base + many])]
 
     def depth_sum(g):
         base, first, many, size = groups[g]
@@ -413,7 +423,7 @@
             for k in range(1, nz):
                 grad = grad + recv_z[k - 1, pl.ds(base // nz, size)].astype(F32)
         full[mine] = grad.astype(BF16)
-        return [per_output(grad), per_output(grad * std[mine]), per_output(grad * grad)]
+        return per_output(grad * grad)
 
     def gather_start(g):
         base, first, many, size = groups[g]
@@ -457,7 +467,7 @@
     for g in range(1, len(groups)):
         rows_chunk(g)
     gather_y_start(1)
-    depth_start(0)
+    linear = [depth_start(0)]
     gather_x_start(0)
     load_more.wait()
     shift_faces()
@@ -497,33 +507,41 @@
 
         lax.fori_loop(0, ex // planes, dx_step, 0)
 
+    for g in range(1, len(groups)):
+        if g != depth_first:
+            linear.append(depth_start(g))
+    depth_middle()
+    gather_y_start(2)
     gather_wait(0)
     dx_pass(0)
-    for g in range(1, len(groups)):
-        if g != depth_first:
-            depth_start(g)
-    depth_middle()
-    gather_y_start(2)
     late = [g for g in range(len(groups)) if g != depth_first]
     late.append(depth_first)
-    sums = None
+    flat = (me["gx"] * ny + me["gy"]) * nz + me["gz"]
+
+    def everywhere(span, n):
+        mine = total_in.at[flat, span]
+        for dz in sorted(range(nz), key=lambda k: -min(k, nz - k)):
+            for dx in range(nx):
+                for dy in range(ny):
+                    if dx or dy or dz:
+                        where = {"gx": peer("gx", dx), "gy": peer("gy", dy), "gz": peer("gz", dz)}
+                        remote(stats.at[1, span], mine, t_send.at[n], t_recv.at[n], where).start()
+
+    squares = None
     for g in late:
         new = depth_sum(g)
+        squares = new if squares is None else squares + new
         if g == 1:
             gather_x_start(1)
-        sums = new if sums is None else [a + b for a, b in zip(sums, new)]
+            linear.append(middle_sums())
+            for n in range(2):
+                stats[1, n] = sum(pair[n] for pair in linear)
+            everywhere(pl.ds(0, 2), 0)
         if g != late[-1]:
             gather_start(g)
-    for n in range(3):
-        stats[1, n] = sums[n]
-    flat = (me["gx"] * ny + me["gy"]) * nz + me["gz"]
+    stats[1, 2] = squares
     total_in[flat] = stats[1]
-    for dz in sorted(range(nz), key=lambda k: -min(k, nz - k)):
-        for dx in range(nx):
-            for dy in range(ny):
-                if dx or dy or dz:
-                    where = {"gx": peer("gx", dx), "gy": peer("gy", dy), "gz": peer("gz", dz)}
-                    remote(stats.at[1], total_in.at[flat], t_send.at[0], t_recv.at[0], where).start()
+    everywhere(pl.ds(2, 1), 1)
     gather_start(late[-1])
     gather_x_start(2)
     gather_wait(1)
@@ -540,13 +558,18 @@
     departed(recv_z, g_send.at[0])
     departed(std_all.at[0, pl.ds(0, ny - 1)], ay_send.at[0])
     departed(std_all.at[pl.ds(0, nx - 1)], ax_send.at[0])
-    others = total_in.at[pl.ds(0, nx * ny * nz - 1)]
-    departed(others, t_send.at[0])
-    arrived(others, t_recv.at[0])
-    sums = total_in[0]
+    others = [total_in.at[pl.ds(0, nx * ny * nz - 1), pl.ds(0, 2)], total_in.at[pl.ds(0, nx * ny * nz - 1), pl.ds(2, 1)]]
+    departed(others[0], t_send.at[0])
+    departed(others[1], t_send.at[1])
+    arrived(others[0], t_recv.at[0])
+    sums = total_in[0, 0:2]
     for k in range(1, nx * ny * nz):
-        sums = sums + total_in[k]
-    sum_grad, sum_cross, sum_square = sums[0], sums[1], sums[2]
+        sums = sums + total_in[k, 0:2]
+    sum_grad, sum_cross = sums[0], sums[1]
+    arrived(others[1], t_recv.at[1])
+    sum_square = total_in[0, 2]
+    for k in range(1, nx * ny * nz):
+        sum_square = sum_square + total_in[k, 2]
     mean_grad = sum_grad / fan_count
     mean_cross = sum_cross / fan_count
     spread = sum_square - 2.0 * mean_grad * sum_grad - 2.0 * mean_cross * sum_cross
@@ -624,7 +647,7 @@
         pltpu.VMEM((stat_slots, 3, 1, chan), F32),
         pltpu.VMEM((nx * ny * nz, 3, 1, chan), F32),
         dma((4,)), *pair(4, 4), *pair(1, many), *pair(2, many), *pair(2, many), *pair(1, 1), *pair(1, 3), *pair(1, 3),
-        *pair(1, 1), *pair(1, 1),
+        *pair(1, 1), *pair(2, 2),
     ]
     vmem = pl.BlockSpec(memory_space=pltpu.VMEM)
     anywhere = pl.BlockSpec(memory_space=pl.ANY)

time: 26.8 us -> 26.5 us (0.989)
  Pallas kernels: 26 us -> 25.7 us
where the time goes in v7:
time: 26.5 us; the launch traced here: 26.4 us
  Pallas kernels  25.7 us (97%)
  between operations  0.64 us (2%)
    pallas_call x1, Pallas kernels, on_device(): pl.pallas_call(functools.partial(kernel, dims), out_shape=(pltpu.VMEM(cot...  24.8 us
    pallas_call x1, Pallas kernels, on_device(): pl.pallas_call(functools.partial(finish_kernel, nz), out_shape=(jax.Shape...  0.88 us

profile of v7, /device:TPU:0, one launch (start us, length us, event | category | flops | bytes accessed | tf_op | source)
XLA Modules:
  0.0 26.4 jit_solution(13372991607193367083)
XLA Ops:
  0.6 24.8 %shard_map.50 = (bf16[8,16,16,128]{3,2,1,0:T(8,128)(2,1)S(1)}, bf16[32,16,128]{2,1,0:T(8,128)(2,1)S(1)}, f32[32,16,128]{2,1,0:T(8,128)S(1)}, f32[8,128]{1,0:T(8,128)S(1)}) custom-call(f32[27,16,128]{2,1,0:T(8,128)} %bitcast.2, bf16[8,16,16,128]{3,2,1,0:T(8,128)(2,1)} %in_hbm.1, bf16[8,16,16,128]{3,2,1,0:T(8,128)(2,1)} %cot_hbm.1), custom_call_target="tpu_custom_call" | custom-call | tf_op jit(solution)/shard_map/pallas_call | solution.py:655
  25.5 0.9 %shard_map.51 = (bf16[8,16,16,128]{3,2,1,0:T(8,128)(2,1)}, f32[27,16,128]{2,1,0:T(8,128)}) custom-call(bf16[8,16,16,128]{3,2,1,0:T(8,128)(2,1)S(1)} %get-tuple-element.8.dx_in, bf16[32,16,128]{2,1,0:T(8,128)(2,1)S(1)} %get-tuple-element.9.full, f32[32,16,128]{2,1,0:T(8,128)S(1)} %get-tuple-element.10.std, f32[8,128]{1,0:T(8,128)S(1)} %get-tuple-element.11.coef_ref), custom_call_target="tpu_custom_call" | custom-call | tf_op jit(solution)/shard_map/pallas_call | solution.py:670

commit v8 on v7

--- a/solution.py
+++ b/solution.py
@@ -587,15 +587,17 @@
 
 
 def finish_kernel(nz, dx_in, full, std, coef_ref, dx_hbm, wg_hbm, wg_ref, sem):
-    out_dx = pltpu.make_async_copy(dx_in, dx_hbm, sem.at[0])
-    out_dx.start()
+    for x in range(dx_in.shape[0]):
+        pltpu.make_async_copy(dx_in.at[x], dx_hbm.at[x], sem.at[0]).start()
     factor, mean_grad, mean_cross = coef_ref[0:1], coef_ref[1:2], coef_ref[2:3]
-    for t, slot in tap_slots(nz):
+    third = wg_ref.shape[0] // 3
+    for t, slot in sorted(tap_slots(nz)):
         wg_ref[t] = factor * (full[slot].astype(F32) - mean_grad - std[slot] * mean_cross)
-    out_wg = pltpu.make_async_copy(wg_ref, wg_hbm, sem.at[1])
-    out_wg.start()
-    out_wg.wait()
-    out_dx.wait()
+        if t % third == third - 1:
+            span = pl.ds(t + 1 - third, third)
+            pltpu.make_async_copy(wg_ref.at[span], wg_hbm.at[span], sem.at[1]).start()
+    pltpu.make_async_copy(dx_in, dx_hbm, sem.at[0]).wait()
+    pltpu.make_async_copy(wg_ref, wg_hbm, sem.at[1]).wait()
 
 
 def on_device(dims, raw_weight, inputs, cotangent):

time: 26.5 us -> 26.5 us (level)
  no operation moved by 1% of the time
where the time goes in v8:
time: 26.5 us; the launch traced here: 26.3 us
  Pallas kernels  25.7 us (97%)
  between operations  0.64 us (2%)
    pallas_call x1, Pallas kernels, on_device(): pl.pallas_call(functools.partial(kernel, dims), out_shape=(pltpu.VMEM(cot...  24.8 us
    pallas_call x1, Pallas kernels, on_device(): pl.pallas_call(functools.partial(finish_kernel, nz), out_shape=(jax.Shape...  0.87 us

profile of v8, /device:TPU:0, one launch (start us, length us, event | category | flops | bytes accessed | tf_op | source)
XLA Modules:
  0.0 26.3 jit_solution(5778771515155450662)
XLA Ops:
  0.6 24.8 %shard_map.50 = (bf16[8,16,16,128]{3,2,1,0:T(8,128)(2,1)S(1)}, bf16[32,16,128]{2,1,0:T(8,128)(2,1)S(1)}, f32[32,16,128]{2,1,0:T(8,128)S(1)}, f32[8,128]{1,0:T(8,128)S(1)}) custom-call(f32[27,16,128]{2,1,0:T(8,128)} %bitcast.2, bf16[8,16,16,128]{3,2,1,0:T(8,128)(2,1)} %in_hbm.1, bf16[8,16,16,128]{3,2,1,0:T(8,128)(2,1)} %cot_hbm.1), custom_call_target="tpu_custom_call" | custom-call | tf_op jit(solution)/shard_map/pallas_call | solution.py:657
  25.5 0.9 %shard_map.51 = (bf16[8,16,16,128]{3,2,1,0:T(8,128)(2,1)}, f32[27,16,128]{2,1,0:T(8,128)}) custom-call(bf16[8,16,16,128]{3,2,1,0:T(8,128)(2,1)S(1)} %get-tuple-element.8.dx_in, bf16[32,16,128]{2,1,0:T(8,128)(2,1)S(1)} %get-tuple-element.9.full, f32[32,16,128]{2,1,0:T(8,128)S(1)} %get-tuple-element.10.std, f32[8,128]{1,0:T(8,128)S(1)} %get-tuple-element.11.coef_ref), custom_call_target="tpu_custom_call" | custom-call | tf_op jit(solution)/shard_map/pallas_call | solution.py:672
